TPU v7x, 32 devices: a whole 2x2x4 slice. The times are simulated.
32 devices in a mesh: mp: 2 (over core), dev: 16 (over z, y, x).
Axes of the slice: x: 2, y: 2, z: 4, core: 2. Of those that a mesh axis runs over, the one named last changes fastest.
Arguments:
- spectrum: float32 [1024, 8192], P(None, ('mp', 'dev')), may hold values from 0.05 to 1
- water_mask: int32 [8192], P(('mp', 'dev')), may hold values 0 or 1
- courant: float32 [2, 1024], replicated, may hold values from 0.05 to 0.3
- stencil_sign: int32 [2, 1024], replicated, may hold values from 0 to 1
- quad_index: int32 [4, 1024, 2], replicated, may hold values from 0 to 1023
- quad_weight: float32 [4, 1024, 2], replicated, may hold values from 0.2 to 1
- nonlinear: float32 [1024], replicated, may hold values from 0.01 to 0.1
- stokes_table: bfloat16 [128, 1024], replicated, may hold values from -0.1875 to 0.1875
- point_index: int32 [4, 8192], P(None, ('mp', 'dev')), may hold values from 0 to 4095, as said below
- point_weight: float32 [4, 8192], P(None, ('mp', 'dev')), may hold values from 0.1 to 0.4
- ocean_index: int32 [4, 4096], P(None, ('mp', 'dev')), may hold values from 0 to 8191, as said below
- ocean_weight: float32 [4, 4096], P(None, ('mp', 'dev')), may hold values from 0.1 to 0.4
- currents: float32 [2, 64, 4096], P(None, None, ('mp', 'dev')), may hold values from -3 to 3
- coriolis: float32 [4096], P(('mp', 'dev')), may hold values from 0.2 to 0.6
- mixing: float32 [64], replicated, may hold values from 0.05 to 0.2
- surface_weights: float32 [64], replicated, may hold values from 0.005 to 0.05
Outputs:
- spectrum_out: float32 [1024, 8192], P(None, ('mp', 'dev'))
- currents_out: float32 [2, 64, 4096], P(None, None, ('mp', 'dev'))
Inputs may be any that keep to these rules, and one draw needn't show every extreme that they name: `point_index`: entry j of point p names an ocean cell in row p // 256 plus -1, 0 or 1 and column (p % 256) // 2 plus -1, 0 or 1, both wrapping. `ocean_index`: entry j of cell c names a wave point in row c // 128 plus -1, 0 or 1 and column 2 (c % 128) plus -2 to 3, both wrapping.
All inputs are finite; a program needn't handle non-finite values. No bound on the sum of `water_mask` on one device may be relied on, other than what follows from the above.
Results may differ from a plain program's by a relative error of at most 0.0003.
The roundings to bfloat16 on the way count: a program that leaves them out, or rounds other values in their place, can miss the bound.
Values sent between devices are 32-bit elements; how exact they have to be, the bound alone decides.
A program may use at most 64 MiB of HBM per device.

v0:
```python
import jax
import jax.numpy as jnp
from jax import lax
from jax.experimental import pallas as pl
from jax.experimental.pallas import tpu as pltpu
from jax.sharding import PartitionSpec as P

STEPS = 2
OCEAN_STEP = 0.5
COMM = 8
BLOCKS = 4
MESH = pl.DeviceIdType.MESH
HIGH = lax.Precision.HIGHEST


def wave_kernel(
    spec, wet, courant, sign, qidx, qwt, nonlinear, table, pidx, pwt, oidx, owt,
    currents, coriolis, mixing, sweight,
    spec_out, cur_out,
    araw, cols, quad, near, far, adv, advb, mid, midb, state,
    sflow, shalo, zhalo, obuf, ohalo, ptab, otab, dbuf, dhalo, dself, tan,
    sem1s, sem1r, sem2s, sem2r, ssend, srecv, zsend, zrecv, osend, orecv, dsend, drecv,
):
    comps, points = spec.shape
    cells = coriolis.shape[1]
    levels = mixing.shape[1]
    dev_count = lax.axis_size("dev")
    total = lax.axis_size("mp") * dev_count
    pos = lax.axis_index("mp") * dev_count + lax.axis_index("dev")
    odd = lax.rem(pos, 2)
    up = lax.rem(pos + 1, total)
    down = lax.rem(pos + total - 1, total)
    up2 = lax.rem(pos + 2, total)
    down2 = lax.rem(pos + total - 2, total)
    partner = pos + 1 - 2 * odd
    far_to = lax.rem(pos + 2 - 4 * odd + total, total)

    def where_is(p):
        return (lax.div(p, dev_count), lax.rem(p, dev_count))

    def remote(src, dst, ssem, rsem, p):
        return pltpu.make_async_remote_copy(
            src_ref=src, dst_ref=dst, send_sem=ssem, recv_sem=rsem,
            device_id=where_is(p), device_id_type=MESH,
        )

    size = comps // COMM

    def rows(c):
        return pl.ds(pl.multiple_of(c * size, size), size)

    def swap(step, c):
        src = spec if step == 0 else mid
        return remote(src.at[rows(c)], near.at[step, rows(c)], sem1s.at[step, c], sem1r.at[step, c], partner)

    def relay(step, c):
        return remote(near.at[step, rows(c)], far.at[step, rows(c)], sem2s.at[step, c], sem2r.at[step, c], far_to)

    def pair(src_up, src_down, halo, ssem, rsem, step):
        return (
            remote(src_up, halo.at[step, 0], ssem.at[step, 0], rsem.at[step, 0], up),
            remote(src_down, halo.at[step, 1], ssem.at[step, 1], rsem.at[step, 1], down),
        )

    def surface_pair(step):
        return pair(sflow.at[step], sflow.at[step], shalo, ssend, srecv, step)

    def zonal_pair(step):
        src = currents.at[0] if step == 0 else state.at[0]
        return pair(src, src, zhalo, zsend, zrecv, step)

    def index_pair():
        return pair(obuf, obuf, ohalo, osend, orecv, 0)

    def drift_pair(step):
        return pair(dbuf.at[step, 0], dbuf.at[step, 1], dhalo, dsend, drecv, step)

    def start(copies):
        for copy in copies:
            copy.start()

    def received(copies):
        for copy in copies:
            copy.wait_recv()

    def sent(copies):
        for copy in copies:
            copy.wait_send()

    def each(low, high, body):
        def run(c, carry):
            body(c)
            return carry

        lax.fori_loop(low, high, run, 0)

    barrier = pltpu.get_barrier_semaphore()
    for p in (up, down, up2, down2):
        pl.semaphore_signal(barrier, inc=1, device_id=where_is(p), device_id_type=MESH)
    pl.semaphore_wait(barrier, 4)

    each(0, COMM, lambda c: swap(0, c).start())
    start(zonal_pair(0))
    obuf[0:4, :] = oidx[...].astype(jnp.float32)
    obuf[4:8, :] = owt[...]

    araw[...] = jnp.zeros_like(araw)
    araw[0:2, :] = courant[...]
    araw[2:4, :] = (2 * sign[...] - 1).astype(jnp.float32)
    araw[4:5, :] = nonlinear[...]
    araw[5:6, 0:levels] = mixing[...]
    araw[6:7, 0:levels] = sweight[...]
    for j in range(4):
        araw[8 + 2 * j : 10 + 2 * j, :] = qidx[j].astype(jnp.float32)
        araw[16 + 2 * j : 18 + 2 * j, :] = qwt[j]
    cols[...] = jnp.transpose(araw[...])
    sflow[...] = jnp.zeros_like(sflow)
    level_mix = cols[0:levels, 5:6]
    level_weight = cols[0:levels, 6:7]

    def surface(source, step):
        for a in range(2):
            sflow[step, a : a + 1, :] = jnp.sum(level_weight * source[a], axis=0, keepdims=True)

    surface(currents, 0)
    start(index_pair())
    start(surface_pair(0))

    lanes = lax.broadcasted_iota(jnp.int32, (32, comps), 1).astype(jnp.float32)

    def build_quad(c):
        for sub in range(size // 32):
            at = pl.ds(pl.multiple_of(c * size + sub * 32, 32), 32)
            col = cols[at, :]
            for j in range(4):
                one = jnp.where(col[:, 8 + 2 * j : 9 + 2 * j] == lanes, col[:, 16 + 2 * j : 17 + 2 * j], 0.0)
                two = jnp.where(col[:, 9 + 2 * j : 10 + 2 * j] == lanes, col[:, 17 + 2 * j : 18 + 2 * j], 0.0)
                quad[j, at, :] = (one + two).astype(jnp.bfloat16)

    def forward(step):
        def body(c):
            swap(step, c).wait_recv()
            relay(step, c).start()

        return body

    def first(c):
        build_quad(c)
        forward(0)(c)

    each(0, COMM, first)

    slots = lax.broadcasted_iota(jnp.int32, (cells, points), 0)
    for q, owner in enumerate((down, pos, up)):
        acc = jnp.zeros((cells, points), jnp.float32)
        for j in range(4):
            acc = acc + jnp.where(pidx[j : j + 1, :] - owner * cells == slots, pwt[j : j + 1, :], 0.0)
        ptab[q] = acc
    received(index_pair())
    oslots = lax.broadcasted_iota(jnp.int32, (points, cells), 0).astype(jnp.float32)
    base = (pos * points).astype(jnp.float32)
    for q in range(3):
        source = obuf[...] if q == 2 else ohalo[0, q]
        acc = jnp.zeros((points, cells), jnp.float32)
        for j in range(4):
            acc = acc + jnp.where(source[j : j + 1, :] - base == oslots, source[4 + j : 5 + j, :], 0.0)
        otab[q] = acc

    parity = (1 - 2 * odd).astype(jnp.float32)

    def flow(step):
        received(surface_pair(step))
        total_flow = jnp.dot(shalo[step, 0], ptab[0], precision=HIGH, preferred_element_type=jnp.float32)
        total_flow += jnp.dot(sflow[step], ptab[1], precision=HIGH, preferred_element_type=jnp.float32)
        total_flow += jnp.dot(shalo[step, 1], ptab[2], precision=HIGH, preferred_element_type=jnp.float32)
        tan[...] = jnp.tanh(total_flow)

    def advect(step):
        source = spec if step == 0 else mid

        def body(c):
            relay(step, c).wait_recv()
            at = rows(c)
            own = source[at, :]
            col = cols[at, :]
            sense_x = col[:, 2:3]
            sense_y = col[:, 3:4]
            behind_x = jnp.where(sense_x > 0, pltpu.roll(own, 1, 1), pltpu.roll(own, points - 1, 1))
            behind_y = jnp.where(sense_y * parity > 0, far[step, at, :], near[step, at, :])
            speed_x = col[:, 0:1] * (1.0 + 0.5 * (sense_x * tan[0:1, :]))
            speed_y = col[:, 1:2] * (1.0 + 0.5 * (sense_y * tan[1:2, :]))
            value = own - speed_x * (own - behind_x) - speed_y * (own - behind_y)
            adv[at, :] = value
            advb[at, :] = value.astype(jnp.bfloat16)

        each(0, COMM, body)

    wide = comps // BLOCKS
    wet_row = wet[...].astype(jnp.float32)

    def source_block(step):
        target = mid if step == 0 else spec_out

        def body(r):
            at = pl.ds(pl.multiple_of(r * wide, wide), wide)
            terms = [
                jnp.dot(quad[j, at, :], advb[...], preferred_element_type=jnp.float32) for j in range(4)
            ]
            value = adv[at, :]
            total_sum = terms[0] + terms[1] + terms[2] + terms[3]
            pair_sum = terms[0] * terms[1] + terms[2] * terms[3]
            new = wet_row * (value + cols[at, 4:5] * (value * value * total_sum - value * pair_sum))
            target[at, :] = new
            midb[at, :] = new.astype(jnp.bfloat16)

        return body

    def drift_parts(step):
        stokes = jnp.dot(table[...], midb[...], preferred_element_type=jnp.float32)
        ahead, behind = drift_pair(step)
        dbuf[step, 0] = jnp.dot(stokes, otab[1], precision=HIGH, preferred_element_type=jnp.float32)
        ahead.start()
        dbuf[step, 1] = jnp.dot(stokes, otab[0], precision=HIGH, preferred_element_type=jnp.float32)
        behind.start()
        dself[...] = jnp.dot(stokes, otab[2], precision=HIGH, preferred_element_type=jnp.float32)

    level_row = lax.broadcasted_iota(jnp.int32, (levels, cells), 0)

    def mix(w):
        above = jnp.where(level_row == 0, w, pltpu.roll(w, 1, 0))
        below = jnp.where(level_row == levels - 1, w, pltpu.roll(w, levels - 1, 0))
        return level_mix * (above - 2.0 * w + below)

    def ocean(step):
        source = currents if step == 0 else state
        target = state if step == 0 else cur_out
        received(zonal_pair(step))
        u, v = source[0], source[1]
        rot = coriolis[...]
        turn = 0.5 * (pltpu.roll(v, cells - 1, 1) - pltpu.roll(v, 1, 1)) - 0.5 * (zhalo[step, 1] - zhalo[step, 0])
        mix_u, mix_v = mix(u), mix(v)
        received(drift_pair(step))
        drift = dself[...] + dhalo[step, 0] + dhalo[step, 1]
        drift_x, drift_y = drift[0:levels], drift[levels : 2 * levels]
        new_u = u + OCEAN_STEP * (rot * (v + drift_y) + turn * drift_y + mix_u)
        new_v = v + OCEAN_STEP * (-rot * (u + drift_x) - turn * drift_x + mix_v)
        target[0] = new_u
        target[1] = new_v

    flow(0)
    advect(0)
    source_block(0)(0)
    per = COMM // BLOCKS
    each(0, per, lambda c: swap(1, c).start())
    each(1, BLOCKS, source_block(0))
    drift_parts(0)
    each(per, COMM, lambda c: swap(1, c).start())
    each(0, COMM - 3, forward(1))
    ocean(0)
    surface(state, 1)
    start(surface_pair(1))
    start(zonal_pair(1))
    each(COMM - 3, COMM, forward(1))
    flow(1)
    advect(1)
    each(0, BLOCKS, source_block(1))
    drift_parts(1)
    ocean(1)

    sent(index_pair())
    for step in range(STEPS):
        each(0, COMM, lambda c: swap(step, c).wait_send())
        each(0, COMM, lambda c: relay(step, c).wait_send())
        sent(surface_pair(step))
        sent(zonal_pair(step))
        sent(drift_pair(step))


def local(
    spectrum, water_mask, courant, stencil_sign, quad_index, quad_weight, nonlinear, stokes_table,
    point_index, point_weight, ocean_index, ocean_weight, currents, coriolis, mixing, surface_weights,
):
    comps, points = spectrum.shape
    levels, cells = currents.shape[1:]
    f32, bf16 = jnp.float32, jnp.bfloat16
    vm = pl.BlockSpec(memory_space=pltpu.VMEM)
    dma = pltpu.SemaphoreType.DMA
    scratch = [
        pltpu.VMEM((128, comps), f32),
        pltpu.VMEM((comps, 128), f32),
        pltpu.VMEM((4, comps, comps), bf16),
        pltpu.VMEM((STEPS, comps, points), f32),
        pltpu.VMEM((STEPS, comps, points), f32),
        pltpu.VMEM((comps, points), f32),
        pltpu.VMEM((comps, points), bf16),
        pltpu.VMEM((comps, points), f32),
        pltpu.VMEM((comps, points), bf16),
        pltpu.VMEM((2, levels, cells), f32),
        pltpu.VMEM((STEPS, 8, cells), f32),
        pltpu.VMEM((STEPS, 2, 8, cells), f32),
        pltpu.VMEM((STEPS, 2, levels, cells), f32),
        pltpu.VMEM((8, cells), f32),
        pltpu.VMEM((1, 2, 8, cells), f32),
        pltpu.VMEM((3, cells, points), f32),
        pltpu.VMEM((3, points, cells), f32),
        pltpu.VMEM((STEPS, 2, 2 * levels, cells), f32),
        pltpu.VMEM((STEPS, 2, 2 * levels, cells), f32),
        pltpu.VMEM((2 * levels, cells), f32),
        pltpu.VMEM((8, points), f32),
        dma((STEPS, COMM)),
        dma((STEPS, COMM)),
        dma((STEPS, COMM)),
        dma((STEPS, COMM)),
    ] + [dma((n, 2)) for n in (STEPS, STEPS, STEPS, STEPS, 1, 1, STEPS, STEPS)]
    return pl.pallas_call(
        wave_kernel,
        out_shape=(
            pltpu.VMEM((comps, points), f32),
            pltpu.VMEM(currents.shape, f32),
        ),
        in_specs=[vm] * 16,
        out_specs=(vm, vm),
        scratch_shapes=scratch,
        compiler_params=pltpu.CompilerParams(
            collective_id=0, has_side_effects=True, vmem_limit_bytes=56 * 1024 * 1024
        ),
    )(
        spectrum,
        water_mask.reshape(1, points),
        courant,
        stencil_sign,
        quad_index.transpose(0, 2, 1),
        quad_weight.transpose(0, 2, 1),
        nonlinear.reshape(1, comps),
        stokes_table,
        point_index,
        point_weight,
        ocean_index,
        ocean_weight,
        currents,
        coriolis.reshape(1, cells),
        mixing.reshape(1, levels),
        surface_weights.reshape(1, levels),
    )


def solution(mesh):
    ring = P(("mp", "dev"))
    split = P(None, ("mp", "dev"))
    deep = P(None, None, ("mp", "dev"))
    return jax.shard_map(
        local,
        mesh=mesh,
        in_specs=(
            split, ring, P(), P(), P(), P(), P(), P(), split, split, split, split, deep, ring, P(), P(),
        ),
        out_specs=(split, deep),
        check_vma=False,
    )
```

profile of v0, /device:TPU:1, one launch (start us, length us, event | category | flops | bytes accessed | tf_op | source)
XLA Modules:
  0.0 83.6 jit_solution(2591963251407553469)
XLA Ops:
  0.6 81.4 %shard_map.167 = (f32[1024,256]{1,0:T(8,128)S(1)}, f32[2,64,128]{2,1,0:T(8,128)S(1)}) custom-call(f32[1024,256]{1,0:T(8,128)} %spec.1, s32[1,256]{1,0:T(1,128)} %bitcast.10, f32[2,1024]{1,0:T(2,128)} %courant.1, s32[2,1024]{1,0:T(2,128)} %sign.1, s32[4,2,1024]{2,1,0:T(2,128)} %bitcast.7, f32[4,2,1024]{2,1,0:T(2,128)} %bitcast.8, f32[1,1024]{1,0:T(1,128)} %bitcast.9, ...), custom_call_target="tpu_custom_call" | custom-call | tf_op jit(solution)/shard_map/pallas_call | solution.py:315
  82.0 1.0 %copy.20 = f32[1024,256]{1,0:T(8,128)} copy(f32[1024,256]{1,0:T(8,128)S(1)} %get-tuple-element.2) | data formatting | bytes 2097152
  83.0 0.6 copy.21
where the time goes:
time: 84.2 us; the launch traced here: 83.6 us
  Pallas kernels  81.4 us (97%)
  local copies, waits for them, and re-layouts  1.6 us (2%)
    pallas_call x1, Pallas kernels, local(): pl.pallas_call(wave_kernel, out_shape=(pltpu.VMEM((comps, points), f32),...  81.4 us

commit v1 on v0

v1 whole, which is shorter than its diff:
```python
import jax
import jax.numpy as jnp
from jax import lax
from jax.experimental import pallas as pl
from jax.experimental.pallas import tpu as pltpu
from jax.sharding import PartitionSpec as P

STEPS = 2
OCEAN_STEP = 0.5
TEAM = 4
COMM = 8
KPARTS = 4
MESH = pl.DeviceIdType.MESH
F32, BF16 = jnp.float32, jnp.bfloat16


def split(x):
    high = x.astype(BF16)
    return high, (x - high.astype(F32)).astype(BF16)


def dot(a, b):
    return jnp.dot(a, b, preferred_element_type=F32)


def dot_split(x, table_high, table_low):
    high, low = split(x)
    return dot(high, table_high) + (dot(low, table_high) + dot(high, table_low))


def wave_kernel(
    spec, wet, courant, sign, qidx, qwt, nonlinear, table, pidx, pwt, oidx, owt,
    currents, coriolis, mixing, sweight,
    spec_out, cur_out,
    araw, cols, lraw, quad, pk, pk2, rx, zpk, zin, ex, exin, edge, adv, advb, acc, mid, midb, state,
    mbuf, meta, bmeta, osm, orx, sbuf, srx, sall, zhalo, ptab, btab, otab, dm, drx, dbuf, dhalo, dself, tan,
    rxs, rxr, zs, zr, es, er, fs, fr, ms, mr, os_, or_, ss, sr, ds_, dr, us, ur, hs, hr,
):
    comps, points = spec.shape
    cells = coriolis.shape[1]
    levels = mixing.shape[1]
    dev_count = lax.axis_size("dev")
    total = lax.axis_size("mp") * dev_count
    pos = lax.axis_index("mp") * dev_count + lax.axis_index("dev")
    b = lax.rem(pos, TEAM)
    base = pos - b
    width = points // TEAM
    window = cells // TEAM
    size = comps // COMM
    half = size // 2
    lanes = 2 * width

    def wrap(p):
        return lax.rem(p + total, total)

    up, down = wrap(pos + 1), wrap(pos - 1)
    ahead, behind = wrap(pos + TEAM), wrap(pos - TEAM)
    mates = [lax.rem(b + i, TEAM) for i in range(1, TEAM)]

    def remote(src, dst, ssem, rsem, p):
        return pltpu.make_async_remote_copy(
            src_ref=src, dst_ref=dst, send_sem=ssem, recv_sem=rsem,
            device_id=(lax.div(p, dev_count), lax.rem(p, dev_count)), device_id_type=MESH,
        )

    def span(c, n):
        return pl.ds(pl.multiple_of(c * n, n), n)

    def rows(c):
        return span(c, size)

    def halves(c):
        return span(c, half)

    def each(low, high, body):
        def run(c, carry):
            body(c)
            return carry

        lax.fori_loop(low, high, run, 0)

    def start(copies):
        for copy in copies:
            copy.start()

    def received(copies):
        for copy in copies:
            copy.wait_recv()

    def sent(copies):
        for copy in copies:
            copy.wait_send()

    def piece_out(step, c):
        src = pk if step == 0 else pk2
        return [
            remote(src.at[d, halves(c)], rx.at[step, b, halves(c)], rxs.at[step, i, c], rxr.at[step, b, c], base + d)
            for i, d in enumerate(mates)
        ]

    def piece_in(step, c):
        src = pk if step == 0 else pk2
        return [
            remote(src.at[d, halves(c)], rx.at[step, d, halves(c)], rxs.at[step, i, c], rxr.at[step, d, c], base + d)
            for i, d in enumerate(mates)
        ]

    def halo(step, c):
        low = rx.at[0, TEAM - 1, halves(c)] if step == 0 else zpk.at[0, halves(c)]
        high = rx.at[0, 0, halves(c)] if step == 0 else zpk.at[1, halves(c)]
        return [
            remote(low, zin.at[step, 0, halves(c)], zs.at[step, 0, c], zr.at[step, 0, c], ahead),
            remote(high, zin.at[step, 1, halves(c)], zs.at[step, 1, c], zr.at[step, 1, c], behind),
        ]

    def edges_out():
        return [remote(ex.at[0], exin.at[b], es.at[i], er.at[b], base + d) for i, d in enumerate(mates)]

    def edges_in():
        return [remote(ex.at[0], exin.at[d], es.at[i], er.at[d], base + d) for i, d in enumerate(mates)]

    right, left = base + mates[0], base + mates[2]

    def sides():
        return [
            remote(ex.at[1], exin.at[TEAM], fs.at[0], fr.at[0], right),
            remote(ex.at[1], exin.at[TEAM + 1], fs.at[1], fr.at[1], left),
        ]

    def meta_out():
        return [remote(mbuf, meta.at[b], ms.at[i], mr.at[b], base + d) for i, d in enumerate(mates)]

    def meta_in():
        return [remote(mbuf, meta.at[d], ms.at[i], mr.at[d], base + d) for i, d in enumerate(mates)]

    def row_out(step):
        src, dst, ssem, rsem = (osm, orx, os_, or_) if step == 0 else (sbuf, srx, ss, sr)
        inner = [remote(src, dst.at[b + 1], ssem.at[i], rsem.at[b + 1], base + d) for i, d in enumerate(mates)]
        before = [
            remote(src, dst.at[TEAM + 1], ssem.at[3 + k], rsem.at[TEAM + 1], wrap(base - TEAM + k)) for k in range(TEAM)
        ]
        after = [remote(src, dst.at[0], ssem.at[3 + k], rsem.at[0], wrap(base + TEAM + k)) for k in range(TEAM)]
        return inner, before, after

    def row_start(step):
        inner, before, after = row_out(step)

        @pl.when(b == 0)
        def _():
            start(before)

        @pl.when(b == TEAM - 1)
        def _():
            start(after)

        start(inner)

    def row_sent(step):
        inner, before, after = row_out(step)
        sent(inner)

        @pl.when(b == 0)
        def _():
            sent(before)

        @pl.when(b == TEAM - 1)
        def _():
            sent(after)

    def row_in(step):
        src, dst, ssem, rsem = (osm, orx, os_, or_) if step == 0 else (sbuf, srx, ss, sr)
        copies = [remote(src, dst.at[d + 1], ssem.at[i], rsem.at[d + 1], base + d) for i, d in enumerate(mates)]
        copies.append(remote(src, dst.at[0], ssem.at[0], rsem.at[0], ahead))
        copies.append(remote(src, dst.at[TEAM + 1], ssem.at[0], rsem.at[TEAM + 1], behind))
        return copies

    def drift_out():
        copies = [
            remote(dm.at[0], drx.at[TEAM + b], ds_.at[3], dr.at[TEAM + b], wrap(base - 1)),
            remote(dm.at[TEAM + 1], drx.at[TEAM + b], ds_.at[4], dr.at[TEAM + b], wrap(base + TEAM)),
        ]
        return copies + [
            remote(dm.at[d + 1], drx.at[b], ds_.at[i], dr.at[b], base + d) for i, d in enumerate(mates)
        ]

    def drift_in():
        inner = [remote(dm.at[0], drx.at[d], ds_.at[i], dr.at[d], base + d) for i, d in enumerate(mates)]
        outer = [remote(dm.at[0], drx.at[TEAM + k], ds_.at[3], dr.at[TEAM + k], ahead) for k in range(TEAM)]
        return inner, outer

    def zonal_pair(step):
        src = currents.at[0] if step == 0 else state.at[0]
        return [
            remote(src, zhalo.at[step, 0], us.at[step, 0], ur.at[step, 0], up),
            remote(src, zhalo.at[step, 1], us.at[step, 1], ur.at[step, 1], down),
        ]

    def last_pair():
        return [
            remote(dbuf.at[0], dhalo.at[0], hs.at[0], hr.at[0], up),
            remote(dbuf.at[1], dhalo.at[1], hs.at[1], hr.at[1], down),
        ]

    drx[TEAM : 2 * TEAM] = jnp.zeros((TEAM, levels, lanes), F32)
    barrier = pltpu.get_barrier_semaphore()
    partners = [base + d for d in mates]
    partners += [wrap(base - TEAM + k) for k in range(TEAM)] + [wrap(base + TEAM + k) for k in range(TEAM)]
    for p in partners:
        pl.semaphore_signal(
            barrier, inc=1, device_id=(lax.div(p, dev_count), lax.rem(p, dev_count)), device_id_type=MESH
        )

    lane = lax.broadcasted_iota(jnp.int32, (half, lanes), 1)
    low = lane < width

    def even(a, c):
        return jnp.where(low, a, pltpu.roll(c, width, 1))

    def odd(a, c):
        return jnp.where(low, pltpu.roll(a, width, 1), c)

    lane_row = lax.broadcasted_iota(jnp.int32, (8, lanes), 1)
    wide_lane = lax.broadcasted_iota(jnp.int32, (size, lanes), 1)
    rim = lax.rem(wide_lane + 1, width) < 2

    def pack_rim(first, second):
        mixed = jnp.where(rim, first, pltpu.roll(second, 2, 1))
        out = jnp.zeros((8, lanes), F32)
        for g in range(size // 8):
            here = lax.rem(lane_row + 1 - 4 * g + lanes, width) < 4
            part = mixed[8 * g : 8 * g + 8]
            out = jnp.where(here, pltpu.roll(part, 4 * g, 1) if g else part, out)
        return out

    lraw[...] = jnp.zeros_like(lraw)
    lraw[0:1, 0:levels] = mixing[...]
    lraw[1:2, 0:levels] = sweight[...]
    lcols = jnp.transpose(lraw[...])
    level_mix = lcols[0:levels, 0:1]
    level_weight = lcols[0:levels, 1:2]

    def surface(source, dst, at):
        dst[at : at + 8, :] = jnp.zeros((8, cells), F32)
        for a in range(2):
            dst[at + a : at + a + 1, :] = jnp.sum(level_weight * source[a], axis=0, keepdims=True)

    osm[0:4, :] = oidx[...].astype(F32)
    osm[4:8, :] = owt[...]
    surface(currents, osm, 8)
    orx[b + 1] = osm[...]
    mbuf[...] = jnp.zeros_like(mbuf)
    mbuf[0:4, :] = pidx[...].astype(F32)
    mbuf[4:8, :] = pwt[...]
    mbuf[8:9, :] = wet[...].astype(F32)
    meta[b] = mbuf[...]

    def pack_in(c):
        for t in range(2):
            tile = spec[rows(c), t * lanes : (t + 1) * lanes]
            first, second = tile[0:half], tile[half:size]
            pk[2 * t, halves(c), :] = even(first, second)
            pk[2 * t + 1, halves(c), :] = odd(first, second)
        rx[0, b, halves(c), :] = pk[b, halves(c), :]
        ex[0, span(c, 8), :] = pack_rim(spec[rows(c), 0:lanes], spec[rows(c), lanes : 2 * lanes])

    each(0, COMM, pack_in)
    exin[b] = ex[0]
    pl.semaphore_wait(barrier, len(partners))

    row_start(0)
    start(meta_out())
    start(edges_out())
    each(0, COMM, lambda c: start(piece_out(0, c)))
    start(zonal_pair(0))

    araw[...] = jnp.zeros_like(araw)
    araw[0:2, :] = courant[...]
    araw[2:4, :] = (2 * sign[...] - 1).astype(F32)
    araw[4:5, :] = nonlinear[...]
    for j in range(4):
        araw[8 + 2 * j : 10 + 2 * j, :] = qidx[j].astype(F32)
        araw[16 + 2 * j : 18 + 2 * j, :] = qwt[j]
    cols[...] = jnp.transpose(araw[...])
    long_lane = lax.broadcasted_iota(jnp.int32, (32, comps), 1).astype(F32)

    def build_quad(c):
        for sub in range(size // 32):
            at = pl.ds(pl.multiple_of(c * size + sub * 32, 32), 32)
            col = cols[at, :]
            for j in range(4):
                one = jnp.where(col[:, 8 + 2 * j : 9 + 2 * j] == long_lane, col[:, 16 + 2 * j : 17 + 2 * j], 0.0)
                two = jnp.where(col[:, 9 + 2 * j : 10 + 2 * j] == long_lane, col[:, 17 + 2 * j : 18 + 2 * j], 0.0)
                quad[j, at, :] = (one + two).astype(BF16)

    def forward(c):
        received(piece_in(0, c))
        start(halo(0, c))

    def first(c):
        build_quad(2 * c)
        build_quad(2 * c + 1)
        forward(c)

    each(0, COMM // 2, first)

    received(meta_in())
    aside = lax.rem(b, 2)
    for t in range(2):
        pieces = []
        for r in (2 * t, 2 * t + 1):
            tile = meta[r, :, pl.ds(pl.multiple_of(lax.div(b, 2) * lanes, lanes), lanes)]
            pieces.append(jnp.where(aside == r % 2, tile, pltpu.roll(tile, width, 1)))
        bmeta[:, t * lanes : (t + 1) * lanes] = jnp.where(low[0:16], pieces[0], pieces[1])

    received(row_in(0))
    slots = lax.broadcasted_iota(jnp.int32, (cells, points), 0).astype(F32)
    for q in range(TEAM + 2):
        owner = (wrap(base - 1 + q) * cells).astype(F32)
        value = jnp.zeros((cells, points), F32)
        for j in range(4):
            value = value + jnp.where(bmeta[j : j + 1, :] - owner == slots, bmeta[4 + j : 5 + j, :], 0.0)
        ptab[0, q * cells : (q + 1) * cells, :], ptab[1, q * cells : (q + 1) * cells, :] = split(value)

    shift = lax.rem(cells + window // 2 - window * b, cells)
    pointer = lax.broadcasted_iota(jnp.int32, (width, cells), 0).astype(F32)
    for t in range((TEAM + 2) // 2):
        near = pltpu.roll(orx[2 * t, 0:8], shift, 1)
        far = pltpu.roll(orx[2 * t + 1, 0:8], shift, 1)
        both = jnp.where(low[0:8], near, pltpu.roll(far, width, 1))
        for r in range(TEAM):
            origin = ((base + r) * points + width * b).astype(F32)
            value = jnp.zeros((width, cells), F32)
            for j in range(4):
                value = value + jnp.where(both[j : j + 1, :] - origin == pointer, both[4 + j : 5 + j, :], 0.0)
            high_part, low_part = split(value)
            btab[0, r * width : (r + 1) * width, t * lanes : (t + 1) * lanes] = high_part
            btab[1, r * width : (r + 1) * width, t * lanes : (t + 1) * lanes] = low_part

    received(edges_in())
    lane_rim = lax.broadcasted_iota(jnp.int32, (size // 2, lanes), 1)
    turn4 = lax.rem(lane_rim, 4)
    upper = lane_rim >= width - 1

    def pick(values):
        return jnp.where(b == 0, values[0], jnp.where(b == 1, values[1], jnp.where(b == 2, values[2], values[3])))

    last = width - 1
    from_left = pick((1, last, lanes - 1, last + 2))
    from_right = pick((width, 2, width + 2, 0))
    to_left = (last, lanes - 1, last + 2, 1)
    to_right = (0, width, 2, width + 2)
    on_left = (
        (turn4 == 3) & upper & (lane_rim < lanes - 1),
        (turn4 == 3) & ((lane_rim < width - 1) | (lane_rim == lanes - 1)),
        (turn4 == 1) & upper,
        (turn4 == 1) & ~upper,
    )
    on_right = ((turn4 == 0) & ~upper, (turn4 == 0) & upper, (turn4 == 2) & ~upper, (turn4 == 2) & upper)
    merged = jnp.zeros((size // 2, lanes), F32)
    for r in range(TEAM):
        merged = jnp.where(on_left[r], pltpu.roll(exin[r], lax.rem(to_left[r] - from_left + lanes, lanes), 1), merged)
        merged = jnp.where(on_right[r], pltpu.roll(exin[r], lax.rem(to_right[r] - from_right + lanes, lanes), 1), merged)
    edge[0] = merged

    def flow(step):
        for q in range(TEAM + 2):
            sall[:, q * cells : (q + 1) * cells] = orx[q, 8:16] if step == 0 else srx[q]
        tan[...] = jnp.tanh(dot_split(sall[...], ptab[0], ptab[1]))

    flow(0)

    lane_half = lax.rem(lane, width)
    at_first, at_last = lane_half == 0, lane_half == width - 1

    def advect(step, c):
        received(halo(step, c))
        rim_row = edge[step, span(c, 8), :]
        out = []
        for sub in range(2):
            at = pl.ds(pl.multiple_of(c * size + sub * half, half), half)
            col = cols[at, :]
            if step == 0:
                join = odd if sub else even
                own = [join(rx[0, 2 * t, halves(c), :], rx[0, 2 * t + 1, halves(c), :]) for t in range(2)]
            else:
                own = [mid[at, t * lanes : (t + 1) * lanes] for t in range(2)]
            turned = [pltpu.roll(x, width, 1) for x in own]
            below, above = zin[step, 0, halves(c), :], zin[step, 1, halves(c), :]
            if sub:
                below = pltpu.roll(below, width, 1)
            else:
                above = pltpu.roll(above, width, 1)
            middle = jnp.where(low, turned[0], turned[1])
            north = (jnp.where(low, below, turned[0]), middle)
            south = (middle, jnp.where(low, turned[1], above))
            groups = range(sub * half // 8, (sub + 1) * half // 8)
            spin = [
                jnp.concatenate([pltpu.roll(rim_row, (k - 4 * g) % lanes, 1) for g in groups], axis=0)
                for k in (width + 1, width - 1, width - 3)
            ]
            sense_x, sense_y = col[:, 2:3], col[:, 3:4]
            values = []
            for t in range(2):
                x = own[t]
                west = jnp.where(at_first, spin[t], pltpu.roll(x, 1, 1))
                east = jnp.where(at_last, spin[t + 1], pltpu.roll(x, lanes - 1, 1))
                behind_x = jnp.where(sense_x > 0, west, east)
                behind_y = jnp.where(sense_y > 0, north[t], south[t])
                lane_at = slice(t * lanes, (t + 1) * lanes)
                speed_x = col[:, 0:1] * (1.0 + 0.5 * (sense_x * tan[0:1, lane_at]))
                speed_y = col[:, 1:2] * (1.0 + 0.5 * (sense_y * tan[1:2, lane_at]))
                values.append(x - speed_x * (x - behind_x) - speed_y * (x - behind_y))
            out.append(values)
        return out

    def keep(c, values):
        for sub in range(2):
            at = pl.ds(pl.multiple_of(c * size + sub * half, half), half)
            for t in range(2):
                adv[at, t * lanes : (t + 1) * lanes] = values[sub][t]
                advb[at, t * lanes : (t + 1) * lanes] = values[sub][t].astype(BF16)

    deep = comps // KPARTS

    def multiply(part):
        k_at = slice(part * deep, (part + 1) * deep)

        def body(i):
            j, at = lax.div(i, KPARTS), span(lax.rem(i, KPARTS), deep)
            value = dot(quad[j, at, k_at], advb[k_at, :])
            if part:
                value = value + acc[j, at, :]
            acc[j, at, :] = value

        each(0, 4 * KPARTS, body)

    def source(step, wet_row):
        target = mid if step == 0 else spec_out
        k_at = slice(comps - deep, comps)

        def body(c):
            at = rows(c)
            terms = [acc[j, at, :] + dot(quad[j, at, k_at], advb[k_at, :]) for j in range(4)]
            value = adv[at, :]
            total_sum = terms[0] + terms[1] + terms[2] + terms[3]
            pair_sum = terms[0] * terms[1] + terms[2] * terms[3]
            new = wet_row * (value + cols[at, 4:5] * (value * value * total_sum - value * pair_sum))
            target[at, :] = new
            midb[at, :] = new.astype(BF16)
            if step == 0:
                ex[1, span(c, 8), :] = pack_rim(new[:, 0:lanes], new[:, lanes : 2 * lanes])
                zpk[0, halves(c), :] = odd(new[0:half, lanes : 2 * lanes], new[half:size, lanes : 2 * lanes])
                zpk[1, halves(c), :] = even(new[0:half, 0:lanes], new[half:size, 0:lanes])

        each(0, COMM, body)

    level_row = lax.broadcasted_iota(jnp.int32, (levels, cells), 0)

    def mix(w):
        above = jnp.where(level_row == 0, w, pltpu.roll(w, 1, 0))
        below = jnp.where(level_row == levels - 1, w, pltpu.roll(w, levels - 1, 0))
        return level_mix * (above - 2.0 * w + below)

    def ocean(step, drift):
        before = currents if step == 0 else state
        target = state if step == 0 else cur_out
        received(zonal_pair(step))
        u, v = before[0], before[1]
        rot = coriolis[...]
        turn = 0.5 * (pltpu.roll(v, cells - 1, 1) - pltpu.roll(v, 1, 1)) - 0.5 * (zhalo[step, 1] - zhalo[step, 0])
        mix_u, mix_v = mix(u), mix(v)
        drift_x, drift_y = drift()
        target[0] = u + OCEAN_STEP * (rot * (v + drift_y) + turn * drift_y + mix_u)
        target[1] = v + OCEAN_STEP * (-rot * (u + drift_x) - turn * drift_x + mix_v)

    for c in range(COMM // 2):
        forward(COMM // 2 + c)
        if c < 2:
            for k in (2 * c, 2 * c + 1):
                keep(k, advect(0, k))
            multiply(c)
        else:
            keep(c + 2, advect(0, c + 2))
    multiply(2)

    oslots = lax.broadcasted_iota(jnp.int32, (points, cells), 0).astype(F32)
    origin = (pos * points).astype(F32)
    for q in range(3):
        value = jnp.zeros((points, cells), F32)
        for j in range(4):
            value = value + jnp.where(
                orx[b + q, j : j + 1, :] - origin == oslots, orx[b + q, 4 + j : 5 + j, :], 0.0
            )
        otab[q, 0], otab[q, 1] = split(value)

    for c in (COMM - 2, COMM - 1):
        keep(c, advect(0, c))
    source(0, bmeta[8:9, :])

    stokes = dot(table[...], midb[...])
    parts = dot_split(stokes, btab[0], btab[1])
    for t in range((TEAM + 2) // 2):
        zonal = parts[0:levels, t * lanes : (t + 1) * lanes]
        merid = parts[levels : 2 * levels, t * lanes : (t + 1) * lanes]
        dm[2 * t], dm[2 * t + 1] = even(zonal, merid), odd(zonal, merid)
    start(drift_out())
    drx[b] = dm[b + 1]
    start(sides())
    each(0, 3, lambda c: start(halo(1, c)))

    def team_drift():
        inner, outer = drift_in()
        received(inner)

        @pl.when((b == 0) | (b == TEAM - 1))
        def _():
            received(outer)

        drift_x = jnp.zeros((levels, cells), F32)
        drift_y = jnp.zeros((levels, cells), F32)
        for s in range(TEAM):
            part = drx[s] + drx[TEAM + s]
            to = (window * s - window // 2) % cells
            drift_x += pltpu.roll(jnp.where(low, part, 0.0), to, 1)
            drift_y += pltpu.roll(jnp.where(low, pltpu.roll(part, width, 1), 0.0), to, 1)
        return drift_x, drift_y

    ocean(0, team_drift)
    surface(state, sbuf, 0)
    row_start(1)
    srx[b + 1] = sbuf[...]
    each(3, COMM, lambda c: start(halo(1, c)))
    received(sides())
    edge[1] = jnp.where(lax.rem(lane_rim, 2) == 1, exin[TEAM], exin[TEAM + 1])
    received(row_in(1))
    flow(1)

    def give(c):
        values = advect(1, c)
        for t in range(2):
            pk2[2 * t, halves(c), :] = even(values[0][t], values[1][t])
            pk2[2 * t + 1, halves(c), :] = odd(values[0][t], values[1][t])
        start(piece_out(1, c))
        rx[1, b, halves(c), :] = pk2[b, halves(c), :]

    def take(c):
        received(piece_in(1, c))
        values = []
        for join in (even, odd):
            values.append([join(rx[1, 2 * t, halves(c), :], rx[1, 2 * t + 1, halves(c), :]) for t in range(2)])
        keep(c, values)

    each(0, 3, give)
    for c in range(3, COMM):
        give(c)
        take(c - 3)
        if c == COMM - 1:
            start(zonal_pair(1))
        if (c - 3) % 2:
            multiply((c - 3) // 2)
    take(COMM - 3)
    multiply(2)
    take(COMM - 2)
    take(COMM - 1)
    source(1, wet[...].astype(F32))

    stokes = dot(table[...], midb[...])
    copies = last_pair()
    dbuf[0] = dot_split(stokes, otab[2, 0], otab[2, 1])
    copies[0].start()
    dbuf[1] = dot_split(stokes, otab[0, 0], otab[0, 1])
    copies[1].start()
    dself[...] = dot_split(stokes, otab[1, 0], otab[1, 1])

    def last_drift():
        received(last_pair())
        drift = dself[...] + dhalo[0] + dhalo[1]
        return drift[0:levels], drift[levels : 2 * levels]

    ocean(1, last_drift)

    sent(meta_out())
    sent(edges_out())
    sent(sides())
    sent(drift_out())
    sent(last_pair())
    for step in range(STEPS):
        row_sent(step)
        sent(zonal_pair(step))
        each(0, COMM, lambda c: sent(piece_out(step, c)))
        each(0, COMM, lambda c: sent(halo(step, c)))


def local(
    spectrum, water_mask, courant, stencil_sign, quad_index, quad_weight, nonlinear, stokes_table,
    point_index, point_weight, ocean_index, ocean_weight, currents, coriolis, mixing, surface_weights,
):
    comps, points = spectrum.shape
    levels, cells = currents.shape[1:]
    lanes = points // 2
    packed = comps // 2
    rim = comps // 16
    vm = pl.BlockSpec(memory_space=pltpu.VMEM)
    dma = pltpu.SemaphoreType.DMA

    def f32(*shape):
        return pltpu.VMEM(shape, F32)

    def bf16(*shape):
        return pltpu.VMEM(shape, BF16)

    scratch = [
        f32(128, comps),
        f32(comps, 128),
        f32(128, 128),
        bf16(4, comps, comps),
        f32(TEAM, packed, lanes),
        f32(TEAM, packed, lanes),
        f32(STEPS, TEAM, packed, lanes),
        f32(2, packed, lanes),
        f32(STEPS, 2, packed, lanes),
        f32(STEPS, rim, lanes),
        f32(TEAM + 2, rim, lanes),
        f32(STEPS, rim, lanes),
        f32(comps, points),
        bf16(comps, points),
        f32(4, comps, points),
        f32(comps, points),
        bf16(comps, points),
        f32(2, levels, cells),
        f32(16, points),
        f32(TEAM, 16, points),
        f32(16, points),
        f32(16, cells),
        f32(TEAM + 2, 16, cells),
        f32(8, cells),
        f32(TEAM + 2, 8, cells),
        f32(8, (TEAM + 2) * cells),
        f32(STEPS, 2, levels, cells),
        bf16(2, (TEAM + 2) * cells, points),
        bf16(2, points, (TEAM + 2) // 2 * lanes),
        bf16(3, 2, points, cells),
        f32(TEAM + 2, levels, lanes),
        f32(2 * TEAM, levels, lanes),
        f32(2, 2 * levels, cells),
        f32(2, 2 * levels, cells),
        f32(2 * levels, cells),
        f32(8, points),
        dma((STEPS, 3, COMM)),
        dma((STEPS, TEAM, COMM)),
        dma((STEPS, 2, COMM)),
        dma((STEPS, 2, COMM)),
        dma((3,)),
        dma((TEAM,)),
        dma((2,)),
        dma((2,)),
        dma((3,)),
        dma((TEAM,)),
        dma((3 + TEAM,)),
        dma((TEAM + 2,)),
        dma((3 + TEAM,)),
        dma((TEAM + 2,)),
        dma((5,)),
        dma((2 * TEAM,)),
        dma((STEPS, 2)),
        dma((STEPS, 2)),
        dma((2,)),
        dma((2,)),
    ]
    return pl.pallas_call(
        wave_kernel,
        out_shape=(
            pltpu.VMEM((comps, points), F32),
            pltpu.VMEM(currents.shape, F32),
        ),
        in_specs=[vm] * 16,
        out_specs=(vm, vm),
        scratch_shapes=scratch,
        compiler_params=pltpu.CompilerParams(
            collective_id=0, has_side_effects=True, vmem_limit_bytes=56 * 1024 * 1024
        ),
    )(
        spectrum,
        water_mask.reshape(1, points),
        courant,
        stencil_sign,
        quad_index.transpose(0, 2, 1),
        quad_weight.transpose(0, 2, 1),
        nonlinear.reshape(1, comps),
        stokes_table,
        point_index,
        point_weight,
        ocean_index,
        ocean_weight,
        currents,
        coriolis.reshape(1, cells),
        mixing.reshape(1, levels),
        surface_weights.reshape(1, levels),
    )


def solution(mesh):
    ring = P(("mp", "dev"))
    split_last = P(None, ("mp", "dev"))
    deep = P(None, None, ("mp", "dev"))
    return jax.shard_map(
        local,
        mesh=mesh,
        in_specs=(
            split_last, ring, P(), P(), P(), P(), P(), P(), split_last, split_last, split_last, split_last, deep,
            ring, P(), P(),
        ),
        out_specs=(split_last, deep),
        check_vma=False,
    )
```

time: 84.2 us -> 77.4 us (0.919)
  Pallas kernels: 81.4 us -> 75 us
    pallas_call x1, Pallas kernels: 81.4 us -> 75 us  [local(): pl.pallas_call(wave_kernel, out_shape=(pltpu.VMEM((comps, points), F32),...]
where the time goes in v1:
time: 77.4 us; the launch traced here: 77.2 us
  Pallas kernels  75 us (97%)
  local copies, waits for them, and re-layouts  1.6 us (2%)
    pallas_call x1, Pallas kernels, local(): pl.pallas_call(wave_kernel, out_shape=(pltpu.VMEM((comps, points), F32),...  75 us
    unnamed x2, local copies, waits for them, and re-layouts  1.6 us

profile of v1, /device:TPU:1, one launch (start us, length us, event | category | flops | bytes accessed | tf_op | source)
XLA Modules:
  0.0 77.2 jit_solution(2484058214195968097)
XLA Ops:
  0.6 75.0 %shard_map.167 = (f32[1024,256]{1,0:T(8,128)S(1)}, f32[2,64,128]{2,1,0:T(8,128)S(1)}) custom-call(f32[1024,256]{1,0:T(8,128)} %spec.1, s32[1,256]{1,0:T(1,128)} %bitcast.10, f32[2,1024]{1,0:T(2,128)} %courant.1, s32[2,1024]{1,0:T(2,128)} %sign.1, s32[4,2,1024]{2,1,0:T(2,128)} %bitcast.7, f32[4,2,1024]{2,1,0:T(2,128)} %bitcast.8, f32[1,1024]{1,0:T(1,128)} %bitcast.9, ...), custom_call_target="tpu_custom_call" | custom-call | tf_op jit(solution)/shard_map/pallas_call | solution.py:670
  75.6 1.0 %copy.20 = f32[1024,256]{1,0:T(8,128)} copy(f32[1024,256]{1,0:T(8,128)S(1)} %get-tuple-element.2) | data formatting | bytes 2097152
  76.6 0.6 copy.21

commit v2 on v1

--- a/solution.py
+++ b/solution.py
@@ -50,6 +50,8 @@
     half = size // 2
     lanes = 2 * width
 
+    none = lax.div(pos, total)
+
     def wrap(p):
         return lax.rem(p + total, total)
 
@@ -94,14 +96,14 @@
     def piece_out(step, c):
         src = pk if step == 0 else pk2
         return [
-            remote(src.at[d, halves(c)], rx.at[step, b, halves(c)], rxs.at[step, i, c], rxr.at[step, b, c], base + d)
+            remote(src.at[d, halves(c)], rx.at[step, b, halves(c)], rxs.at[step, i], rxr.at[step, b, c], base + d)
             for i, d in enumerate(mates)
         ]
 
     def piece_in(step, c):
         src = pk if step == 0 else pk2
         return [
-            remote(src.at[d, halves(c)], rx.at[step, d, halves(c)], rxs.at[step, i, c], rxr.at[step, d, c], base + d)
+            remote(src.at[d, halves(c)], rx.at[step, d, halves(c)], rxs.at[step, i], rxr.at[step, d, c], base + d)
             for i, d in enumerate(mates)
         ]
 
@@ -109,9 +111,21 @@
         low = rx.at[0, TEAM - 1, halves(c)] if step == 0 else zpk.at[0, halves(c)]
         high = rx.at[0, 0, halves(c)] if step == 0 else zpk.at[1, halves(c)]
         return [
-            remote(low, zin.at[step, 0, halves(c)], zs.at[step, 0, c], zr.at[step, 0, c], ahead),
-            remote(high, zin.at[step, 1, halves(c)], zs.at[step, 1, c], zr.at[step, 1, c], behind),
-        ]
+            remote(low, zin.at[step, 0, halves(c)], zs.at[step, 0], zr.at[step, 0, c], ahead),
+            remote(high, zin.at[step, 1, halves(c)], zs.at[step, 1], zr.at[step, 1, c], behind),
+        ]
+
+    def all_out(step):
+        src = pk if step == 0 else pk2
+        copies = [
+            remote(src.at[d], rx.at[step, b], rxs.at[step, i], rxr.at[step, b, 0], base + d)
+            for i, d in enumerate(mates)
+        ]
+        low_from = rx.at[0, TEAM - 1] if step == 0 else zpk.at[0]
+        high_from = rx.at[0, 0] if step == 0 else zpk.at[1]
+        copies.append(remote(low_from, zin.at[step, 0], zs.at[step, 0], zr.at[step, 0, 0], ahead))
+        copies.append(remote(high_from, zin.at[step, 1], zs.at[step, 1], zr.at[step, 1, 0], behind))
+        return copies
 
     def edges_out():
         return [remote(ex.at[0], exin.at[b], es.at[i], er.at[b], base + d) for i, d in enumerate(mates)]
@@ -261,48 +275,53 @@
             pk[2 * t, halves(c), :] = even(first, second)
             pk[2 * t + 1, halves(c), :] = odd(first, second)
         rx[0, b, halves(c), :] = pk[b, halves(c), :]
+        start(piece_out(0, c))
+
+    def rim_in(c):
         ex[0, span(c, 8), :] = pack_rim(spec[rows(c), 0:lanes], spec[rows(c), lanes : 2 * lanes])
 
-    each(0, COMM, pack_in)
+    each(0, COMM, rim_in)
     exin[b] = ex[0]
     pl.semaphore_wait(barrier, len(partners))
 
+    each(0, 1, pack_in)
     row_start(0)
     start(meta_out())
+    each(1, 2, pack_in)
     start(edges_out())
-    each(0, COMM, lambda c: start(piece_out(0, c)))
+    each(2, COMM, pack_in)
     start(zonal_pair(0))
-
     araw[...] = jnp.zeros_like(araw)
     araw[0:2, :] = courant[...]
     araw[2:4, :] = (2 * sign[...] - 1).astype(F32)
     araw[4:5, :] = nonlinear[...]
     for j in range(4):
-        araw[8 + 2 * j : 10 + 2 * j, :] = qidx[j].astype(F32)
-        araw[16 + 2 * j : 18 + 2 * j, :] = qwt[j]
+        index, weight = qidx[j], qwt[j]
+        twice = index[0:1] == index[1:2]
+        araw[8 + 2 * j : 10 + 2 * j, :] = index.astype(F32)
+        araw[16 + 2 * j : 17 + 2 * j, :] = jnp.where(twice, weight[0:1] + weight[1:2], weight[0:1])
+        araw[17 + 2 * j : 18 + 2 * j, :] = weight[1:2]
     cols[...] = jnp.transpose(araw[...])
     long_lane = lax.broadcasted_iota(jnp.int32, (32, comps), 1).astype(F32)
 
     def build_quad(c):
         for sub in range(size // 32):
-            at = pl.ds(pl.multiple_of(c * size + sub * 32, 32), 32)
-            col = cols[at, :]
+            begin = pl.multiple_of(c * size + sub * 32, 32)
+            col = cols[pl.ds(begin, 32), :]
             for j in range(4):
-                one = jnp.where(col[:, 8 + 2 * j : 9 + 2 * j] == long_lane, col[:, 16 + 2 * j : 17 + 2 * j], 0.0)
                 two = jnp.where(col[:, 9 + 2 * j : 10 + 2 * j] == long_lane, col[:, 17 + 2 * j : 18 + 2 * j], 0.0)
-                quad[j, at, :] = (one + two).astype(BF16)
+                one = jnp.where(col[:, 8 + 2 * j : 9 + 2 * j] == long_lane, col[:, 16 + 2 * j : 17 + 2 * j], two)
+                quad[pl.ds(begin + j * comps, 32), :] = one.astype(BF16)
 
     def forward(c):
         received(piece_in(0, c))
         start(halo(0, c))
 
-    def first(c):
-        build_quad(2 * c)
-        build_quad(2 * c + 1)
-        forward(c)
-
-    each(0, COMM // 2, first)
-
+    each(0, COMM // 2, build_quad)
+    forward(0)
+    each(COMM // 2, COMM - 1, build_quad)
+    forward(1)
+    each(COMM - 1, COMM, build_quad)
     received(meta_in())
     aside = lax.rem(b, 2)
     for t in range(2):
@@ -336,6 +355,7 @@
             btab[0, r * width : (r + 1) * width, t * lanes : (t + 1) * lanes] = high_part
             btab[1, r * width : (r + 1) * width, t * lanes : (t + 1) * lanes] = low_part
 
+    forward(2)
     received(edges_in())
     lane_rim = lax.broadcasted_iota(jnp.int32, (size // 2, lanes), 1)
     turn4 = lax.rem(lane_rim, 4)
@@ -372,50 +392,65 @@
     lane_half = lax.rem(lane, width)
     at_first, at_last = lane_half == 0, lane_half == width - 1
 
-    def advect(step, c):
+    unit = half // 2
+    low_unit = low[0:unit]
+    at_first, at_last = at_first[0:unit], at_last[0:unit]
+
+    def advect(step, c, emit):
         received(halo(step, c))
-        rim_row = edge[step, span(c, 8), :]
-        out = []
+
+        def body(r):
+            packed = pl.ds(pl.multiple_of(c * half + r * unit, unit), unit)
+            turn = lax.rem(lanes - 4 * (unit // 8) * r, lanes)
+            rim_row = pltpu.roll(edge[step, span(c, 8), :], turn, 1)
+            out = []
+            for sub in range(2):
+                at = pl.ds(pl.multiple_of(c * size + sub * half + r * unit, unit), unit)
+                col = cols[at, :]
+                if step == 0:
+                    own = []
+                    for t in range(2):
+                        a, d = rx[0, 2 * t, packed, :], rx[0, 2 * t + 1, packed, :]
+                        if sub:
+                            own.append(jnp.where(low_unit, pltpu.roll(a, width, 1), d))
+                        else:
+                            own.append(jnp.where(low_unit, a, pltpu.roll(d, width, 1)))
+                else:
+                    own = [mid[at, t * lanes : (t + 1) * lanes] for t in range(2)]
+                turned = [pltpu.roll(x, width, 1) for x in own]
+                below, above = zin[step, 0, packed, :], zin[step, 1, packed, :]
+                if sub:
+                    below = pltpu.roll(below, width, 1)
+                else:
+                    above = pltpu.roll(above, width, 1)
+                middle = jnp.where(low_unit, turned[0], turned[1])
+                north = (jnp.where(low_unit, below, turned[0]), middle)
+                south = (middle, jnp.where(low_unit, turned[1], above))
+                groups = range(sub * half // 8, sub * half // 8 + unit // 8)
+                spin = [
+                    jnp.concatenate([pltpu.roll(rim_row, (k - 4 * g) % lanes, 1) for g in groups], axis=0)
+                    for k in (width + 1, width - 1, width - 3)
+                ]
+                sense_x, sense_y = col[:, 2:3], col[:, 3:4]
+                values = []
+                for t in range(2):
+                    x = own[t]
+                    west = jnp.where(at_first, spin[t], pltpu.roll(x, 1, 1))
+                    east = jnp.where(at_last, spin[t + 1], pltpu.roll(x, lanes - 1, 1))
+                    behind_x = jnp.where(sense_x > 0, west, east)
+                    behind_y = jnp.where(sense_y > 0, north[t], south[t])
+                    lane_at = slice(t * lanes, (t + 1) * lanes)
+                    speed_x = col[:, 0:1] * (1.0 + 0.5 * (sense_x * tan[0:1, lane_at]))
+                    speed_y = col[:, 1:2] * (1.0 + 0.5 * (sense_y * tan[1:2, lane_at]))
+                    values.append(x - speed_x * (x - behind_x) - speed_y * (x - behind_y))
+                out.append(values)
+            emit(c, r, out)
+
+        each(0, half // unit, body)
+
+    def keep(c, r, values):
         for sub in range(2):
-            at = pl.ds(pl.multiple_of(c * size + sub * half, half), half)
-            col = cols[at, :]
-            if step == 0:
-                join = odd if sub else even
-                own = [join(rx[0, 2 * t, halves(c), :], rx[0, 2 * t + 1, halves(c), :]) for t in range(2)]
-            else:
-                own = [mid[at, t * lanes : (t + 1) * lanes] for t in range(2)]
-            turned = [pltpu.roll(x, width, 1) for x in own]
-            below, above = zin[step, 0, halves(c), :], zin[step, 1, halves(c), :]
-            if sub:
-                below = pltpu.roll(below, width, 1)
-            else:
-                above = pltpu.roll(above, width, 1)
-            middle = jnp.where(low, turned[0], turned[1])
-            north = (jnp.where(low, below, turned[0]), middle)
-            south = (middle, jnp.where(low, turned[1], above))
-            groups = range(sub * half // 8, (sub + 1) * half // 8)
-            spin = [
-                jnp.concatenate([pltpu.roll(rim_row, (k - 4 * g) % lanes, 1) for g in groups], axis=0)
-                for k in (width + 1, width - 1, width - 3)
-            ]
-            sense_x, sense_y = col[:, 2:3], col[:, 3:4]
-            values = []
-            for t in range(2):
-                x = own[t]
-                west = jnp.where(at_first, spin[t], pltpu.roll(x, 1, 1))
-                east = jnp.where(at_last, spin[t + 1], pltpu.roll(x, lanes - 1, 1))
-                behind_x = jnp.where(sense_x > 0, west, east)
-                behind_y = jnp.where(sense_y > 0, north[t], south[t])
-                lane_at = slice(t * lanes, (t + 1) * lanes)
-                speed_x = col[:, 0:1] * (1.0 + 0.5 * (sense_x * tan[0:1, lane_at]))
-                speed_y = col[:, 1:2] * (1.0 + 0.5 * (sense_y * tan[1:2, lane_at]))
-                values.append(x - speed_x * (x - behind_x) - speed_y * (x - behind_y))
-            out.append(values)
-        return out
-
-    def keep(c, values):
-        for sub in range(2):
-            at = pl.ds(pl.multiple_of(c * size + sub * half, half), half)
+            at = pl.ds(pl.multiple_of(c * size + sub * half + r * unit, unit), unit)
             for t in range(2):
                 adv[at, t * lanes : (t + 1) * lanes] = values[sub][t]
                 advb[at, t * lanes : (t + 1) * lanes] = values[sub][t].astype(BF16)
@@ -426,21 +461,19 @@
         k_at = slice(part * deep, (part + 1) * deep)
 
         def body(i):
-            j, at = lax.div(i, KPARTS), span(lax.rem(i, KPARTS), deep)
-            value = dot(quad[j, at, k_at], advb[k_at, :])
             if part:
-                value = value + acc[j, at, :]
-            acc[j, at, :] = value
-
-        each(0, 4 * KPARTS, body)
+                acc[...] = acc[...] + dot(quad[:, k_at], advb[k_at, :])
+            else:
+                acc[...] = dot(quad[:, k_at], advb[k_at, :])
+
+        each(none, none + 1, body)
 
     def source(step, wet_row):
         target = mid if step == 0 else spec_out
-        k_at = slice(comps - deep, comps)
 
         def body(c):
             at = rows(c)
-            terms = [acc[j, at, :] + dot(quad[j, at, k_at], advb[k_at, :]) for j in range(4)]
+            terms = [acc[pl.ds(pl.multiple_of(j * comps + c * size, size), size), :] for j in range(4)]
             value = adv[at, :]
             total_sum = terms[0] + terms[1] + terms[2] + terms[3]
             pair_sum = terms[0] * terms[1] + terms[2] * terms[3]
@@ -473,19 +506,10 @@
         target[0] = u + OCEAN_STEP * (rot * (v + drift_y) + turn * drift_y + mix_u)
         target[1] = v + OCEAN_STEP * (-rot * (u + drift_x) - turn * drift_x + mix_v)
 
-    for c in range(COMM // 2):
-        forward(COMM // 2 + c)
-        if c < 2:
-            for k in (2 * c, 2 * c + 1):
-                keep(k, advect(0, k))
-            multiply(c)
-        else:
-            keep(c + 2, advect(0, c + 2))
-    multiply(2)
-
     oslots = lax.broadcasted_iota(jnp.int32, (points, cells), 0).astype(F32)
     origin = (pos * points).astype(F32)
-    for q in range(3):
+
+    def last_table(q):
         value = jnp.zeros((points, cells), F32)
         for j in range(4):
             value = value + jnp.where(
@@ -493,8 +517,16 @@
             )
         otab[q, 0], otab[q, 1] = split(value)
 
-    for c in (COMM - 2, COMM - 1):
-        keep(c, advect(0, c))
+    for c in range(3, COMM):
+        forward(c)
+        advect(0, c - 3, keep)
+        if (c - 3) % 2:
+            multiply((c - 3) // 2)
+    advect(0, COMM - 3, keep)
+    multiply(2)
+    advect(0, COMM - 2, keep)
+    advect(0, COMM - 1, keep)
+    multiply(KPARTS - 1)
     source(0, bmeta[8:9, :])
 
     stokes = dot(table[...], midb[...])
@@ -506,7 +538,9 @@
     start(drift_out())
     drx[b] = dm[b + 1]
     start(sides())
-    each(0, 3, lambda c: start(halo(1, c)))
+    each(0, 2, lambda c: start(halo(1, c)))
+    for q in range(3):
+        last_table(q)
 
     def team_drift():
         inner, outer = drift_in()
@@ -529,26 +563,32 @@
     surface(state, sbuf, 0)
     row_start(1)
     srx[b + 1] = sbuf[...]
-    each(3, COMM, lambda c: start(halo(1, c)))
+    each(2, COMM, lambda c: start(halo(1, c)))
     received(sides())
     edge[1] = jnp.where(lax.rem(lane_rim, 2) == 1, exin[TEAM], exin[TEAM + 1])
     received(row_in(1))
     flow(1)
 
+    def stack(c, r, values):
+        packed = pl.ds(pl.multiple_of(c * half + r * unit, unit), unit)
+        for t in range(2):
+            first, second = values[0][t], values[1][t]
+            pk2[2 * t, packed, :] = jnp.where(low_unit, first, pltpu.roll(second, width, 1))
+            pk2[2 * t + 1, packed, :] = jnp.where(low_unit, pltpu.roll(first, width, 1), second)
+
     def give(c):
-        values = advect(1, c)
-        for t in range(2):
-            pk2[2 * t, halves(c), :] = even(values[0][t], values[1][t])
-            pk2[2 * t + 1, halves(c), :] = odd(values[0][t], values[1][t])
+        advect(1, c, stack)
         start(piece_out(1, c))
         rx[1, b, halves(c), :] = pk2[b, halves(c), :]
 
     def take(c):
         received(piece_in(1, c))
-        values = []
-        for join in (even, odd):
-            values.append([join(rx[1, 2 * t, halves(c), :], rx[1, 2 * t + 1, halves(c), :]) for t in range(2)])
-        keep(c, values)
+        for sub, join in enumerate((even, odd)):
+            at = pl.ds(pl.multiple_of(c * size + sub * half, half), half)
+            for t in range(2):
+                value = join(rx[1, 2 * t, halves(c), :], rx[1, 2 * t + 1, halves(c), :])
+                adv[at, t * lanes : (t + 1) * lanes] = value
+                advb[at, t * lanes : (t + 1) * lanes] = value.astype(BF16)
 
     each(0, 3, give)
     for c in range(3, COMM):
@@ -562,6 +602,7 @@
     multiply(2)
     take(COMM - 2)
     take(COMM - 1)
+    multiply(KPARTS - 1)
     source(1, wet[...].astype(F32))
 
     stokes = dot(table[...], midb[...])
@@ -587,8 +628,7 @@
     for step in range(STEPS):
         row_sent(step)
         sent(zonal_pair(step))
-        each(0, COMM, lambda c: sent(piece_out(step, c)))
-        each(0, COMM, lambda c: sent(halo(step, c)))
+        sent(all_out(step))
 
 
 def local(
@@ -613,7 +653,7 @@
         f32(128, comps),
         f32(comps, 128),
         f32(128, 128),
-        bf16(4, comps, comps),
+        bf16(4 * comps, comps),
         f32(TEAM, packed, lanes),
         f32(TEAM, packed, lanes),
         f32(STEPS, TEAM, packed, lanes),
@@ -624,7 +664,7 @@
         f32(STEPS, rim, lanes),
         f32(comps, points),
         bf16(comps, points),
-        f32(4, comps, points),
+        f32(4 * comps, points),
         f32(comps, points),
         bf16(comps, points),
         f32(2, levels, cells),
@@ -646,9 +686,9 @@
         f32(2, 2 * levels, cells),
         f32(2 * levels, cells),
         f32(8, points),
-        dma((STEPS, 3, COMM)),
+        dma((STEPS, 3)),
         dma((STEPS, TEAM, COMM)),
-        dma((STEPS, 2, COMM)),
+        dma((STEPS, 2)),
         dma((STEPS, 2, COMM)),
         dma((3,)),
         dma((TEAM,)),

time: 77.4 us -> 68 us (0.88)
  Pallas kernels: 75 us -> 65.6 us
    pallas_call x1, Pallas kernels: 75 us -> 65.6 us  [local(): pl.pallas_call(wave_kernel, out_shape=(pltpu.VMEM((comps, points), F32),...]
where the time goes in v2:
time: 68 us; the launch traced here: 67.9 us
  Pallas kernels  65.6 us (96%)
  local copies, waits for them, and re-layouts  1.6 us (2%)
    pallas_call x1, Pallas kernels, local(): pl.pallas_call(wave_kernel, out_shape=(pltpu.VMEM((comps, points), F32),...  65.6 us
    unnamed x2, local copies, waits for them, and re-layouts  1.6 us

profile of v2, /device:TPU:1, one launch (start us, length us, event | category | flops | bytes accessed | tf_op | source)
XLA Modules:
  0.0 67.9 jit_solution(11179596772103162868)
XLA Ops:
  0.6 65.6 %shard_map.167 = (f32[1024,256]{1,0:T(8,128)S(1)}, f32[2,64,128]{2,1,0:T(8,128)S(1)}) custom-call(f32[1024,256]{1,0:T(8,128)} %spec.1, s32[1,256]{1,0:T(1,128)} %bitcast.10, f32[2,1024]{1,0:T(2,128)} %courant.1, s32[2,1024]{1,0:T(2,128)} %sign.1, s32[4,2,1024]{2,1,0:T(2,128)} %bitcast.7, f32[4,2,1024]{2,1,0:T(2,128)} %bitcast.8, f32[1,1024]{1,0:T(1,128)} %bitcast.9, ...), custom_call_target="tpu_custom_call" | custom-call | tf_op jit(solution)/shard_map/pallas_call | solution.py:710
  66.3 1.0 %copy.20 = f32[1024,256]{1,0:T(8,128)} copy(f32[1024,256]{1,0:T(8,128)S(1)} %get-tuple-element.2) | data formatting | bytes 2097152
  67.2 0.6 copy.21

commit v3 on v2

--- a/solution.py
+++ b/solution.py
@@ -9,6 +9,8 @@
 OCEAN_STEP = 0.5
 TEAM = 4
 COMM = 8
+EARLY = 4
+INPUTS = 16
 KPARTS = 4
 MESH = pl.DeviceIdType.MESH
 F32, BF16 = jnp.float32, jnp.bfloat16
@@ -28,13 +30,21 @@
     return dot(high, table_high) + (dot(low, table_high) + dot(high, table_low))
 
 
-def wave_kernel(
+def wave_kernel(*refs):
+    given, (spec_out, cur_out), scratch = refs[:INPUTS], refs[INPUTS : INPUTS + 2], refs[INPUTS + 2 :]
+    copied, load_sems, rest = scratch[:INPUTS], scratch[INPUTS], scratch[INPUTS + 1 :]
+    loads = [pltpu.make_async_copy(a, c, load_sems.at[i]) for i, (a, c) in enumerate(zip(given, copied))]
+    wave_body(loads, *copied, spec_out, cur_out, *rest)
+
+
+def wave_body(
+    loads,
     spec, wet, courant, sign, qidx, qwt, nonlinear, table, pidx, pwt, oidx, owt,
     currents, coriolis, mixing, sweight,
     spec_out, cur_out,
-    araw, cols, lraw, quad, pk, pk2, rx, zpk, zin, ex, exin, edge, adv, advb, acc, mid, midb, state,
-    mbuf, meta, bmeta, osm, orx, sbuf, srx, sall, zhalo, ptab, btab, otab, dm, drx, dbuf, dhalo, dself, tan,
-    rxs, rxr, zs, zr, es, er, fs, fr, ms, mr, os_, or_, ss, sr, ds_, dr, us, ur, hs, hr,
+    araw, cols, lraw, quad, pk, pk2, pkb, rx, rxb, zpk, zin, ex, exin, ce, cein, edge, adv, advb, acc, mid, midb, state,
+    mbuf, meta, bmeta, osm, orx, sbuf, srx, sall, zhalo, ptab, rtab, btab, otab, dm, drx, dbuf, dhalo, dself, tan, tanr,
+    rxs, rxr, bs, br, zs, zr, es, er, fs, fr, ms, mr, os_, or_, ss, sr, ds_, dr, us, ur, hs, hr,
 ):
     comps, points = spec.shape
     cells = coriolis.shape[1]
@@ -115,6 +125,21 @@
             remote(high, zin.at[step, 1, halves(c)], zs.at[step, 1], zr.at[step, 1, c], behind),
         ]
 
+    def beside_out(c):
+        return [
+            remote(pkb.at[d, halves(c)], rxb.at[b, halves(c)], bs.at[i], br.at[b, c], base + d)
+            for i, d in enumerate(mates)
+        ]
+
+    def beside_in(c):
+        return [
+            remote(pkb.at[d, halves(c)], rxb.at[d, halves(c)], bs.at[i], br.at[d, c], base + d)
+            for i, d in enumerate(mates)
+        ]
+
+    def beside_all():
+        return [remote(pkb.at[d], rxb.at[b], bs.at[i], br.at[b, 0], base + d) for i, d in enumerate(mates)]
+
     def all_out(step):
         src = pk if step == 0 else pk2
         copies = [
@@ -128,17 +153,17 @@
         return copies
 
     def edges_out():
-        return [remote(ex.at[0], exin.at[b], es.at[i], er.at[b], base + d) for i, d in enumerate(mates)]
+        return [remote(ce.at[d], cein.at[b], es.at[i], er.at[b], base + d) for i, d in enumerate(mates)]
 
     def edges_in():
-        return [remote(ex.at[0], exin.at[d], es.at[i], er.at[d], base + d) for i, d in enumerate(mates)]
+        return [remote(ce.at[d], cein.at[d], es.at[i], er.at[d], base + d) for i, d in enumerate(mates)]
 
     right, left = base + mates[0], base + mates[2]
 
     def sides():
         return [
-            remote(ex.at[1], exin.at[TEAM], fs.at[0], fr.at[0], right),
-            remote(ex.at[1], exin.at[TEAM + 1], fs.at[1], fr.at[1], left),
+            remote(ex.at[1], exin.at[0], fs.at[0], fr.at[0], right),
+            remote(ex.at[1], exin.at[1], fs.at[1], fr.at[1], left),
         ]
 
     def meta_out():
@@ -215,6 +240,7 @@
             remote(dbuf.at[1], dhalo.at[1], hs.at[1], hr.at[1], down),
         ]
 
+    start(loads)
     drx[TEAM : 2 * TEAM] = jnp.zeros((TEAM, levels, lanes), F32)
     barrier = pltpu.get_barrier_semaphore()
     partners = [base + d for d in mates]
@@ -246,27 +272,9 @@
             out = jnp.where(here, pltpu.roll(part, 4 * g, 1) if g else part, out)
         return out
 
-    lraw[...] = jnp.zeros_like(lraw)
-    lraw[0:1, 0:levels] = mixing[...]
-    lraw[1:2, 0:levels] = sweight[...]
-    lcols = jnp.transpose(lraw[...])
-    level_mix = lcols[0:levels, 0:1]
-    level_weight = lcols[0:levels, 1:2]
-
-    def surface(source, dst, at):
-        dst[at : at + 8, :] = jnp.zeros((8, cells), F32)
-        for a in range(2):
-            dst[at + a : at + a + 1, :] = jnp.sum(level_weight * source[a], axis=0, keepdims=True)
-
-    osm[0:4, :] = oidx[...].astype(F32)
-    osm[4:8, :] = owt[...]
-    surface(currents, osm, 8)
-    orx[b + 1] = osm[...]
-    mbuf[...] = jnp.zeros_like(mbuf)
-    mbuf[0:4, :] = pidx[...].astype(F32)
-    mbuf[4:8, :] = pwt[...]
-    mbuf[8:9, :] = wet[...].astype(F32)
-    meta[b] = mbuf[...]
+    for load in loads:
+        load.wait()
+    pl.semaphore_wait(barrier, len(partners))
 
     def pack_in(c):
         for t in range(2):
@@ -277,17 +285,50 @@
         rx[0, b, halves(c), :] = pk[b, halves(c), :]
         start(piece_out(0, c))
 
+    each(0, 1, pack_in)
+    lraw[...] = jnp.zeros_like(lraw)
+    lraw[0:1, 0:levels] = mixing[...]
+    lraw[1:2, 0:levels] = sweight[...]
+    lcols = jnp.transpose(lraw[...])
+    level_mix = lcols[0:levels, 0:1]
+    level_weight = lcols[0:levels, 1:2]
+
+    def surface(source, dst, at):
+        dst[at : at + 8, :] = jnp.zeros((8, cells), F32)
+        for a in range(2):
+            dst[at + a : at + a + 1, :] = jnp.sum(level_weight * source[a], axis=0, keepdims=True)
+
+    osm[0:4, :] = oidx[...].astype(F32)
+    osm[4:8, :] = owt[...]
+    surface(currents, osm, 8)
+    orx[b + 1] = osm[...]
+    row_start(0)
+    mbuf[0:4, :] = pidx[...].astype(F32)
+    mbuf[0:1, :] = (2 * pidx[0:1, :] + wet[...]).astype(F32)
+    mbuf[4:8, :] = pwt[...]
+    meta[b] = mbuf[...]
+    start(meta_out())
+    each(1, 2, pack_in)
+
     def rim_in(c):
         ex[0, span(c, 8), :] = pack_rim(spec[rows(c), 0:lanes], spec[rows(c), lanes : 2 * lanes])
 
     each(0, COMM, rim_in)
-    exin[b] = ex[0]
-    pl.semaphore_wait(barrier, len(partners))
-
-    each(0, 1, pack_in)
-    row_start(0)
-    start(meta_out())
-    each(1, 2, pack_in)
+    last = width - 1
+    from_left = (1, last, lanes - 1, last + 2)
+    from_right = (width, 2, width + 2, 0)
+    quarter = lax.rem(lane_row, 4)
+    ahead_half = lane_row < width
+    for d in range(TEAM):
+        for v in range(COMM // 4):
+            out = jnp.zeros((8, lanes), F32)
+            for k in range(4):
+                part = ex[0, 8 * (4 * v + k) : 8 * (4 * v + k) + 8, :]
+                west = pltpu.roll(part, (k - from_left[d]) % lanes, 1)
+                east = pltpu.roll(part, (width + k - from_right[d]) % lanes, 1)
+                out = jnp.where(quarter == k, jnp.where(ahead_half, west, east), out)
+            ce[d, 8 * v : 8 * v + 8, :] = out
+    cein[b] = ce[b]
     start(edges_out())
     each(2, COMM, pack_in)
     start(zonal_pair(0))
@@ -329,8 +370,12 @@
         for r in (2 * t, 2 * t + 1):
             tile = meta[r, :, pl.ds(pl.multiple_of(lax.div(b, 2) * lanes, lanes), lanes)]
             pieces.append(jnp.where(aside == r % 2, tile, pltpu.roll(tile, width, 1)))
-        bmeta[:, t * lanes : (t + 1) * lanes] = jnp.where(low[0:16], pieces[0], pieces[1])
-
+        bmeta[0:8, t * lanes : (t + 1) * lanes] = jnp.where(low[0:8], pieces[0], pieces[1])
+
+    joined = bmeta[0:1, :]
+    halved = jnp.floor(0.5 * joined)
+    bmeta[8:9, :] = joined - 2.0 * halved
+    bmeta[0:1, :] = halved
     received(row_in(0))
     slots = lax.broadcasted_iota(jnp.int32, (cells, points), 0).astype(F32)
     for q in range(TEAM + 2):
@@ -357,30 +402,25 @@
 
     forward(2)
     received(edges_in())
-    lane_rim = lax.broadcasted_iota(jnp.int32, (size // 2, lanes), 1)
-    turn4 = lax.rem(lane_rim, 4)
-    upper = lane_rim >= width - 1
-
-    def pick(values):
-        return jnp.where(b == 0, values[0], jnp.where(b == 1, values[1], jnp.where(b == 2, values[2], values[3])))
-
-    last = width - 1
-    from_left = pick((1, last, lanes - 1, last + 2))
-    from_right = pick((width, 2, width + 2, 0))
+    lane_rim = lax.broadcasted_iota(jnp.int32, (8 * COMM, lanes), 1)
+    upper = lane_row >= last
     to_left = (last, lanes - 1, last + 2, 1)
     to_right = (0, width, 2, width + 2)
     on_left = (
-        (turn4 == 3) & upper & (lane_rim < lanes - 1),
-        (turn4 == 3) & ((lane_rim < width - 1) | (lane_rim == lanes - 1)),
-        (turn4 == 1) & upper,
-        (turn4 == 1) & ~upper,
+        (quarter == 3) & upper & (lane_row < lanes - 1),
+        (quarter == 3) & ((lane_row < last) | (lane_row == lanes - 1)),
+        (quarter == 1) & upper,
+        (quarter == 1) & ~upper,
     )
-    on_right = ((turn4 == 0) & ~upper, (turn4 == 0) & upper, (turn4 == 2) & ~upper, (turn4 == 2) & upper)
-    merged = jnp.zeros((size // 2, lanes), F32)
-    for r in range(TEAM):
-        merged = jnp.where(on_left[r], pltpu.roll(exin[r], lax.rem(to_left[r] - from_left + lanes, lanes), 1), merged)
-        merged = jnp.where(on_right[r], pltpu.roll(exin[r], lax.rem(to_right[r] - from_right + lanes, lanes), 1), merged)
-    edge[0] = merged
+    on_right = ((quarter == 0) & ~upper, (quarter == 0) & upper, (quarter == 2) & ~upper, (quarter == 2) & upper)
+    for c in range(COMM):
+        v, k = c // 4, c % 4
+        out = jnp.zeros((8, lanes), F32)
+        for r in range(TEAM):
+            part = cein[r, 8 * v : 8 * v + 8, :]
+            out = jnp.where(on_left[r], pltpu.roll(part, (to_left[r] - k) % lanes, 1), out)
+            out = jnp.where(on_right[r], pltpu.roll(part, (to_right[r] - width - k) % lanes, 1), out)
+        edge[0, 8 * c : 8 * c + 8, :] = out
 
     def flow(step):
         for q in range(TEAM + 2):
@@ -392,7 +432,7 @@
     lane_half = lax.rem(lane, width)
     at_first, at_last = lane_half == 0, lane_half == width - 1
 
-    unit = half // 2
+    unit = half
     low_unit = low[0:unit]
     at_first, at_last = at_first[0:unit], at_last[0:unit]
 
@@ -468,6 +508,15 @@
 
         each(none, none + 1, body)
 
+    def halo_out(c):
+        tiles = [mid[rows(c), t * lanes : (t + 1) * lanes] for t in range(2)]
+        zpk[0, halves(c), :] = odd(tiles[1][0:half], tiles[1][half:size])
+        zpk[1, halves(c), :] = even(tiles[0][0:half], tiles[0][half:size])
+        start(halo(1, c))
+
+    def rim_out(c):
+        ex[1, span(c, 8), :] = pack_rim(mid[rows(c), 0:lanes], mid[rows(c), lanes : 2 * lanes])
+
     def source(step, wet_row):
         target = mid if step == 0 else spec_out
 
@@ -480,12 +529,13 @@
             new = wet_row * (value + cols[at, 4:5] * (value * value * total_sum - value * pair_sum))
             target[at, :] = new
             midb[at, :] = new.astype(BF16)
-            if step == 0:
-                ex[1, span(c, 8), :] = pack_rim(new[:, 0:lanes], new[:, lanes : 2 * lanes])
-                zpk[0, halves(c), :] = odd(new[0:half, lanes : 2 * lanes], new[half:size, lanes : 2 * lanes])
-                zpk[1, halves(c), :] = even(new[0:half, 0:lanes], new[half:size, 0:lanes])
-
-        each(0, COMM, body)
+
+        if step == 0:
+            each(0, 1, body)
+            each(0, 1, halo_out)
+            each(1, COMM, body)
+        else:
+            each(0, COMM, body)
 
     level_row = lax.broadcasted_iota(jnp.int32, (levels, cells), 0)
 
@@ -516,6 +566,11 @@
                 orx[b + q, j : j + 1, :] - origin == oslots, orx[b + q, 4 + j : 5 + j, :], 0.0
             )
         otab[q, 0], otab[q, 1] = split(value)
+        owner = (wrap(pos - 1 + q) * cells).astype(F32)
+        value = jnp.zeros((cells, points), F32)
+        for j in range(4):
+            value = value + jnp.where(pidx[j : j + 1, :].astype(F32) - owner == slots, pwt[j : j + 1, :], 0.0)
+        rtab[0, q * cells : (q + 1) * cells, :], rtab[1, q * cells : (q + 1) * cells, :] = split(value)
 
     for c in range(3, COMM):
         forward(c)
@@ -537,8 +592,19 @@
         dm[2 * t], dm[2 * t + 1] = even(zonal, merid), odd(zonal, merid)
     start(drift_out())
     drx[b] = dm[b + 1]
+    def own_out(c):
+        for t in range(2):
+            tile = mid[rows(c), t * lanes : (t + 1) * lanes]
+            first, second = tile[0:half], tile[half:size]
+            pk2[2 * t, halves(c), :] = even(first, second)
+            pk2[2 * t + 1, halves(c), :] = odd(first, second)
+        start(piece_out(1, c))
+        rx[1, b, halves(c), :] = pk2[b, halves(c), :]
+
+    each(1, 3, halo_out)
+    each(0, EARLY, own_out)
+    each(0, COMM, rim_out)
     start(sides())
-    each(0, 2, lambda c: start(halo(1, c)))
     for q in range(3):
         last_table(q)
 
@@ -563,9 +629,33 @@
     surface(state, sbuf, 0)
     row_start(1)
     srx[b + 1] = sbuf[...]
-    each(2, COMM, lambda c: start(halo(1, c)))
+    each(3, COMM, halo_out)
+
+    def beside(c):
+        received(halo(1, c))
+        sides_y = []
+        for sub in range(2):
+            at = pl.ds(pl.multiple_of(c * size + sub * half, half), half)
+            turned = [pltpu.roll(mid[at, t * lanes : (t + 1) * lanes], width, 1) for t in range(2)]
+            below, above = zin[1, 0, halves(c), :], zin[1, 1, halves(c), :]
+            if sub:
+                below = pltpu.roll(below, width, 1)
+            else:
+                above = pltpu.roll(above, width, 1)
+            middle = jnp.where(low, turned[0], turned[1])
+            north = (jnp.where(low, below, turned[0]), middle)
+            south = (middle, jnp.where(low, turned[1], above))
+            sense_y = cols[at, 3:4]
+            sides_y.append([jnp.where(sense_y > 0, north[t], south[t]) for t in range(2)])
+        for t in range(2):
+            pkb[2 * t, halves(c), :] = even(sides_y[0][t], sides_y[1][t])
+            pkb[2 * t + 1, halves(c), :] = odd(sides_y[0][t], sides_y[1][t])
+        start(beside_out(c))
+        rxb[b, halves(c), :] = pkb[b, halves(c), :]
+
+    each(0, EARLY, beside)
     received(sides())
-    edge[1] = jnp.where(lax.rem(lane_rim, 2) == 1, exin[TEAM], exin[TEAM + 1])
+    edge[1] = jnp.where(lax.rem(lane_rim, 2) == 1, exin[0], exin[1])
     received(row_in(1))
     flow(1)
 
@@ -590,19 +680,40 @@
                 adv[at, t * lanes : (t + 1) * lanes] = value
                 advb[at, t * lanes : (t + 1) * lanes] = value.astype(BF16)
 
-    each(0, 3, give)
-    for c in range(3, COMM):
-        give(c)
-        take(c - 3)
-        if c == COMM - 1:
-            start(zonal_pair(1))
-        if (c - 3) % 2:
-            multiply((c - 3) // 2)
-    take(COMM - 3)
-    multiply(2)
-    take(COMM - 2)
-    take(COMM - 1)
-    multiply(KPARTS - 1)
+    def flow_row():
+        own_part = sall[:, pl.ds(pl.multiple_of(b * cells, cells), 3 * cells)]
+        tanr[...] = jnp.tanh(dot_split(own_part, rtab[0], rtab[1]))
+
+    def advance(c):
+        received(piece_in(1, c))
+        received(beside_in(c))
+        for sub, join in enumerate((even, odd)):
+            at = pl.ds(pl.multiple_of(c * size + sub * half, half), half)
+            col = cols[at, :]
+            sense_x, sense_y = col[:, 2:3], col[:, 3:4]
+            own = [join(rx[1, 2 * t, halves(c), :], rx[1, 2 * t + 1, halves(c), :]) for t in range(2)]
+            behind_y = [join(rxb[2 * t, halves(c), :], rxb[2 * t + 1, halves(c), :]) for t in range(2)]
+            forth = [pltpu.roll(x, 1, 1) for x in own]
+            back = [pltpu.roll(x, lanes - 1, 1) for x in own]
+            for t in range(2):
+                x = own[t]
+                west = jnp.where(lane == 0, forth[1 - t], forth[t])
+                east = jnp.where(lane == lanes - 1, back[1 - t], back[t])
+                behind_x = jnp.where(sense_x > 0, west, east)
+                lane_at = slice(t * lanes, (t + 1) * lanes)
+                speed_x = col[:, 0:1] * (1.0 + 0.5 * (sense_x * tanr[0:1, lane_at]))
+                speed_y = col[:, 1:2] * (1.0 + 0.5 * (sense_y * tanr[1:2, lane_at]))
+                value = x - speed_x * (x - behind_x) - speed_y * (x - behind_y[t])
+                adv[at, lane_at] = value
+                advb[at, lane_at] = value.astype(BF16)
+
+    each(EARLY, COMM, give)
+    start(zonal_pair(1))
+    flow_row()
+    for part in range(KPARTS):
+        turn = advance if part < EARLY // 2 else take
+        each(2 * part, 2 * part + 2, turn)
+        multiply(part)
     source(1, wet[...].astype(F32))
 
     stokes = dot(table[...], midb[...])
@@ -620,6 +731,7 @@
 
     ocean(1, last_drift)
 
+    sent(beside_all())
     sent(meta_out())
     sent(edges_out())
     sent(sides())
@@ -656,11 +768,15 @@
         bf16(4 * comps, comps),
         f32(TEAM, packed, lanes),
         f32(TEAM, packed, lanes),
+        f32(TEAM, packed * EARLY // COMM, lanes),
         f32(STEPS, TEAM, packed, lanes),
+        f32(TEAM, packed * EARLY // COMM, lanes),
         f32(2, packed, lanes),
         f32(STEPS, 2, packed, lanes),
         f32(STEPS, rim, lanes),
-        f32(TEAM + 2, rim, lanes),
+        f32(2, rim, lanes),
+        f32(TEAM, rim // 4, lanes),
+        f32(TEAM, rim // 4, lanes),
         f32(STEPS, rim, lanes),
         f32(comps, points),
         bf16(comps, points),
@@ -668,8 +784,8 @@
         f32(comps, points),
         bf16(comps, points),
         f32(2, levels, cells),
-        f32(16, points),
-        f32(TEAM, 16, points),
+        f32(8, points),
+        f32(TEAM, 8, points),
         f32(16, points),
         f32(16, cells),
         f32(TEAM + 2, 16, cells),
@@ -678,6 +794,7 @@
         f32(8, (TEAM + 2) * cells),
         f32(STEPS, 2, levels, cells),
         bf16(2, (TEAM + 2) * cells, points),
+        bf16(2, 3 * cells, points),
         bf16(2, points, (TEAM + 2) // 2 * lanes),
         bf16(3, 2, points, cells),
         f32(TEAM + 2, levels, lanes),
@@ -686,8 +803,11 @@
         f32(2, 2 * levels, cells),
         f32(2 * levels, cells),
         f32(8, points),
+        f32(8, points),
         dma((STEPS, 3)),
         dma((STEPS, TEAM, COMM)),
+        dma((3,)),
+        dma((TEAM, EARLY)),
         dma((STEPS, 2)),
         dma((STEPS, 2, COMM)),
         dma((3,)),
@@ -707,19 +827,7 @@
         dma((2,)),
         dma((2,)),
     ]
-    return pl.pallas_call(
-        wave_kernel,
-        out_shape=(
-            pltpu.VMEM((comps, points), F32),
-            pltpu.VMEM(currents.shape, F32),
-        ),
-        in_specs=[vm] * 16,
-        out_specs=(vm, vm),
-        scratch_shapes=scratch,
-        compiler_params=pltpu.CompilerParams(
-            collective_id=0, has_side_effects=True, vmem_limit_bytes=56 * 1024 * 1024
-        ),
-    )(
+    operands = (
         spectrum,
         water_mask.reshape(1, points),
         courant,
@@ -737,6 +845,20 @@
         mixing.reshape(1, levels),
         surface_weights.reshape(1, levels),
     )
+    scratch = [pltpu.VMEM(x.shape, x.dtype) for x in operands] + [dma((INPUTS,))] + scratch
+    return pl.pallas_call(
+        wave_kernel,
+        out_shape=(
+            pltpu.VMEM((comps, points), F32),
+            pltpu.VMEM(currents.shape, F32),
+        ),
+        in_specs=[pl.BlockSpec(memory_space=pltpu.HBM)] * INPUTS,
+        out_specs=(vm, vm),
+        scratch_shapes=scratch,
+        compiler_params=pltpu.CompilerParams(
+            collective_id=0, has_side_effects=True, vmem_limit_bytes=56 * 1024 * 1024
+        ),
+    )(*operands)
 
 
 def solution(mesh):

time: 68 us -> 63.4 us (0.932)
  Pallas kernels: 65.6 us -> 61 us
    pallas_call x1, Pallas kernels: 65.6 us -> 61 us  [local(): pl.pallas_call(wave_kernel, out_shape=(pltpu.VMEM((comps, points), F32),...]
where the time goes in v3:
time: 63.4 us; the launch traced here: 63.2 us
  Pallas kernels  61 us (96%)
  local copies, waits for them, and re-layouts  1.6 us (3%)
  between operations  0.65 us (1%)
    pallas_call x1, Pallas kernels, local(): pl.pallas_call(wave_kernel, out_shape=(pltpu.VMEM((comps, points), F32),...  61 us
    unnamed x2, local copies, waits for them, and re-layouts  1.6 us

profile of v3, /device:TPU:1, one launch (start us, length us, event | category | flops | bytes accessed | tf_op | source)
XLA Modules:
  0.0 63.2 jit_solution(2301978682965842815)
XLA Ops:
  0.6 61.0 %shard_map.167 = (f32[1024,256]{1,0:T(8,128)S(1)}, f32[2,64,128]{2,1,0:T(8,128)S(1)}) custom-call(f32[1024,256]{1,0:T(8,128)} %refs_0_.1, s32[1,256]{1,0:T(1,128)} %bitcast.10, f32[2,1024]{1,0:T(2,128)} %refs_2_.1, s32[2,1024]{1,0:T(2,128)} %refs_3_.1, s32[4,2,1024]{2,1,0:T(2,128)} %bitcast.7, f32[4,2,1024]{2,1,0:T(2,128)} %bitcast.8, f32[1,1024]{1,0:T(1,128)} %bitcast.9, ...), custom_call_target="tpu_custom_call" | custom-call | tf_op jit(solution)/shard_map/pallas_call | solution.py:849
  61.6 1.0 %copy.20 = f32[1024,256]{1,0:T(8,128)} copy(f32[1024,256]{1,0:T(8,128)S(1)} %get-tuple-element.2) | data formatting | bytes 2097152
  62.6 0.6 copy.21

commit v4 on v3

--- a/solution.py
+++ b/solution.py
@@ -9,7 +9,7 @@
 OCEAN_STEP = 0.5
 TEAM = 4
 COMM = 8
-EARLY = 4
+EARLY = 3
 INPUTS = 16
 KPARTS = 4
 MESH = pl.DeviceIdType.MESH
@@ -103,82 +103,84 @@
         for copy in copies:
             copy.wait_send()
 
+    def spread(src, dst, ssem, rsem):
+        return [remote(src.at[d], dst, ssem, rsem, base + d) for d in mates]
+
+    def gather(src, dst, ssem, rsem, count):
+        return [remote(src.at[0:count], dst.at[0:count], ssem, rsem, base + mates[0])]
+
+    def piece(step, c):
+        return (pk if step == 0 else pk2).at[:, halves(c)], rx.at[step, :, halves(c)]
+
     def piece_out(step, c):
-        src = pk if step == 0 else pk2
+        src, dst = piece(step, c)
+        return spread(src, dst.at[b], rxs.at[step], rxr.at[step, c])
+
+    def piece_in(step, c):
+        src, dst = piece(step, c)
+        return gather(src, dst, rxs.at[step], rxr.at[step, c], TEAM - 1)
+
+    def piece_all(step):
+        return gather(pk if step == 0 else pk2, rx.at[step], rxs.at[step], rxr.at[step, 0], TEAM - 1)
+
+    def halo(step, c):
+        from_low = rx.at[0, TEAM - 1, halves(c)] if step == 0 else zpk.at[0, halves(c)]
+        from_high = rx.at[0, 0, halves(c)] if step == 0 else zpk.at[1, halves(c)]
         return [
-            remote(src.at[d, halves(c)], rx.at[step, b, halves(c)], rxs.at[step, i], rxr.at[step, b, c], base + d)
-            for i, d in enumerate(mates)
+            remote(from_low, zin.at[step, 0, halves(c)], zs.at[step], zr.at[step, c], ahead),
+            remote(from_high, zin.at[step, 1, halves(c)], zs.at[step], zr.at[step, c], behind),
         ]
 
-    def piece_in(step, c):
-        src = pk if step == 0 else pk2
+    def halo_in(step, c):
+        return [remote(zpk.at[:, halves(c)], zin.at[step, :, halves(c)], zs.at[step], zr.at[step, c], ahead)]
+
+    def halo_all(step):
+        return [remote(zpk, zin.at[step], zs.at[step], zr.at[step, 0], ahead)]
+
+    def beside_out(c):
+        return spread(pkb.at[:, halves(c)], rxb.at[b, halves(c)], bs.at[0], br.at[c])
+
+    def beside_in(c):
+        return gather(pkb.at[:, halves(c)], rxb.at[:, halves(c)], bs.at[0], br.at[c], TEAM - 1)
+
+    def beside_all():
+        return gather(pkb, rxb, bs.at[0], br.at[0], TEAM - 1)
+
+    def edges_out():
+        return spread(ce, cein.at[b], es.at[0], er.at[0])
+
+    def edges_in():
+        return gather(ce, cein, es.at[0], er.at[0], TEAM - 1)
+
+    right, left = base + mates[0], base + mates[2]
+
+    later = pl.ds(8 * EARLY, 8 * (COMM - EARLY))
+
+    def sides_out():
         return [
-            remote(src.at[d, halves(c)], rx.at[step, d, halves(c)], rxs.at[step, i], rxr.at[step, d, c], base + d)
-            for i, d in enumerate(mates)
+            remote(ex.at[1, later], exin.at[0, later], fs.at[0], fr.at[0], right),
+            remote(ex.at[1, later], exin.at[1, later], fs.at[0], fr.at[0], left),
         ]
 
-    def halo(step, c):
-        low = rx.at[0, TEAM - 1, halves(c)] if step == 0 else zpk.at[0, halves(c)]
-        high = rx.at[0, 0, halves(c)] if step == 0 else zpk.at[1, halves(c)]
-        return [
-            remote(low, zin.at[step, 0, halves(c)], zs.at[step, 0], zr.at[step, 0, c], ahead),
-            remote(high, zin.at[step, 1, halves(c)], zs.at[step, 1], zr.at[step, 1, c], behind),
+    def sides():
+        return [remote(ex.at[:, later], exin.at[:, later], fs.at[0], fr.at[0], right)]
+
+    def meta_out():
+        return [remote(mbuf, meta.at[b], ms.at[0], mr.at[0], base + d) for d in mates]
+
+    def meta_in():
+        return gather(meta, meta, ms.at[0], mr.at[0], TEAM - 1)
+
+    def row_refs(step):
+        return (osm, orx, os_, or_) if step == 0 else (sbuf, srx, ss, sr)
+
+    def row_out(step):
+        src, dst, ssem, rsem = row_refs(step)
+        inner = [remote(src, dst.at[b + 1], ssem.at[0], rsem.at[0], base + d) for d in mates]
+        before = [
+            remote(src, dst.at[TEAM + 1], ssem.at[1], rsem.at[0], wrap(base - TEAM + k)) for k in range(TEAM)
         ]
-
-    def beside_out(c):
-        return [
-            remote(pkb.at[d, halves(c)], rxb.at[b, halves(c)], bs.at[i], br.at[b, c], base + d)
-            for i, d in enumerate(mates)
-        ]
-
-    def beside_in(c):
-        return [
-            remote(pkb.at[d, halves(c)], rxb.at[d, halves(c)], bs.at[i], br.at[d, c], base + d)
-            for i, d in enumerate(mates)
-        ]
-
-    def beside_all():
-        return [remote(pkb.at[d], rxb.at[b], bs.at[i], br.at[b, 0], base + d) for i, d in enumerate(mates)]
-
-    def all_out(step):
-        src = pk if step == 0 else pk2
-        copies = [
-            remote(src.at[d], rx.at[step, b], rxs.at[step, i], rxr.at[step, b, 0], base + d)
-            for i, d in enumerate(mates)
-        ]
-        low_from = rx.at[0, TEAM - 1] if step == 0 else zpk.at[0]
-        high_from = rx.at[0, 0] if step == 0 else zpk.at[1]
-        copies.append(remote(low_from, zin.at[step, 0], zs.at[step, 0], zr.at[step, 0, 0], ahead))
-        copies.append(remote(high_from, zin.at[step, 1], zs.at[step, 1], zr.at[step, 1, 0], behind))
-        return copies
-
-    def edges_out():
-        return [remote(ce.at[d], cein.at[b], es.at[i], er.at[b], base + d) for i, d in enumerate(mates)]
-
-    def edges_in():
-        return [remote(ce.at[d], cein.at[d], es.at[i], er.at[d], base + d) for i, d in enumerate(mates)]
-
-    right, left = base + mates[0], base + mates[2]
-
-    def sides():
-        return [
-            remote(ex.at[1], exin.at[0], fs.at[0], fr.at[0], right),
-            remote(ex.at[1], exin.at[1], fs.at[1], fr.at[1], left),
-        ]
-
-    def meta_out():
-        return [remote(mbuf, meta.at[b], ms.at[i], mr.at[b], base + d) for i, d in enumerate(mates)]
-
-    def meta_in():
-        return [remote(mbuf, meta.at[d], ms.at[i], mr.at[d], base + d) for i, d in enumerate(mates)]
-
-    def row_out(step):
-        src, dst, ssem, rsem = (osm, orx, os_, or_) if step == 0 else (sbuf, srx, ss, sr)
-        inner = [remote(src, dst.at[b + 1], ssem.at[i], rsem.at[b + 1], base + d) for i, d in enumerate(mates)]
-        before = [
-            remote(src, dst.at[TEAM + 1], ssem.at[3 + k], rsem.at[TEAM + 1], wrap(base - TEAM + k)) for k in range(TEAM)
-        ]
-        after = [remote(src, dst.at[0], ssem.at[3 + k], rsem.at[0], wrap(base + TEAM + k)) for k in range(TEAM)]
+        after = [remote(src, dst.at[0], ssem.at[1], rsem.at[0], wrap(base + TEAM + k)) for k in range(TEAM)]
         return inner, before, after
 
     def row_start(step):
@@ -195,50 +197,48 @@
         start(inner)
 
     def row_sent(step):
-        inner, before, after = row_out(step)
-        sent(inner)
-
-        @pl.when(b == 0)
+        src, dst, ssem, rsem = row_refs(step)
+        sent(gather(dst, dst, ssem.at[0], rsem.at[0], TEAM - 1))
+
+        @pl.when((b == 0) | (b == TEAM - 1))
         def _():
-            sent(before)
-
-        @pl.when(b == TEAM - 1)
-        def _():
-            sent(after)
+            sent(gather(dst, dst, ssem.at[1], rsem.at[0], TEAM))
 
     def row_in(step):
-        src, dst, ssem, rsem = (osm, orx, os_, or_) if step == 0 else (sbuf, srx, ss, sr)
-        copies = [remote(src, dst.at[d + 1], ssem.at[i], rsem.at[d + 1], base + d) for i, d in enumerate(mates)]
-        copies.append(remote(src, dst.at[0], ssem.at[0], rsem.at[0], ahead))
-        copies.append(remote(src, dst.at[TEAM + 1], ssem.at[0], rsem.at[TEAM + 1], behind))
-        return copies
+        src, dst, ssem, rsem = row_refs(step)
+        return gather(dst, dst, ssem.at[0], rsem.at[0], TEAM + 1)
 
     def drift_out():
         copies = [
-            remote(dm.at[0], drx.at[TEAM + b], ds_.at[3], dr.at[TEAM + b], wrap(base - 1)),
-            remote(dm.at[TEAM + 1], drx.at[TEAM + b], ds_.at[4], dr.at[TEAM + b], wrap(base + TEAM)),
+            remote(dm.at[0], drx.at[TEAM + b], ds_.at[0], dr.at[1], wrap(base - 1)),
+            remote(dm.at[TEAM + 1], drx.at[TEAM + b], ds_.at[0], dr.at[1], wrap(base + TEAM)),
         ]
-        return copies + [
-            remote(dm.at[d + 1], drx.at[b], ds_.at[i], dr.at[b], base + d) for i, d in enumerate(mates)
-        ]
+        return copies + [remote(dm.at[d + 1], drx.at[b], ds_.at[0], dr.at[0], base + d) for d in mates]
+
+    def drift_all():
+        return gather(dm, drx, ds_.at[0], dr.at[0], TEAM + 1)
 
     def drift_in():
-        inner = [remote(dm.at[0], drx.at[d], ds_.at[i], dr.at[d], base + d) for i, d in enumerate(mates)]
-        outer = [remote(dm.at[0], drx.at[TEAM + k], ds_.at[3], dr.at[TEAM + k], ahead) for k in range(TEAM)]
-        return inner, outer
-
-    def zonal_pair(step):
+        return gather(dm, drx, ds_.at[0], dr.at[0], TEAM - 1), gather(dm, drx, ds_.at[0], dr.at[1], TEAM)
+
+    def zonal_out(step):
         src = currents.at[0] if step == 0 else state.at[0]
         return [
-            remote(src, zhalo.at[step, 0], us.at[step, 0], ur.at[step, 0], up),
-            remote(src, zhalo.at[step, 1], us.at[step, 1], ur.at[step, 1], down),
+            remote(src, zhalo.at[step, 0], us.at[step], ur.at[step], up),
+            remote(src, zhalo.at[step, 1], us.at[step], ur.at[step], down),
         ]
 
-    def last_pair():
+    def zonal_pair(step):
+        return [remote(currents, zhalo.at[step], us.at[step], ur.at[step], up)]
+
+    def last_out():
         return [
             remote(dbuf.at[0], dhalo.at[0], hs.at[0], hr.at[0], up),
-            remote(dbuf.at[1], dhalo.at[1], hs.at[1], hr.at[1], down),
+            remote(dbuf.at[1], dhalo.at[1], hs.at[0], hr.at[0], down),
         ]
+
+    def last_pair():
+        return [remote(dbuf, dhalo, hs.at[0], hr.at[0], up)]
 
     start(loads)
     drx[TEAM : 2 * TEAM] = jnp.zeros((TEAM, levels, lanes), F32)
@@ -331,7 +331,7 @@
     cein[b] = ce[b]
     start(edges_out())
     each(2, COMM, pack_in)
-    start(zonal_pair(0))
+    start(zonal_out(0))
     araw[...] = jnp.zeros_like(araw)
     araw[0:2, :] = courant[...]
     araw[2:4, :] = (2 * sign[...] - 1).astype(F32)
@@ -437,7 +437,7 @@
     at_first, at_last = at_first[0:unit], at_last[0:unit]
 
     def advect(step, c, emit):
-        received(halo(step, c))
+        received(halo_in(step, c))
 
         def body(r):
             packed = pl.ds(pl.multiple_of(c * half + r * unit, unit), unit)
@@ -601,10 +601,10 @@
         start(piece_out(1, c))
         rx[1, b, halves(c), :] = pk2[b, halves(c), :]
 
-    each(1, 3, halo_out)
-    each(0, EARLY, own_out)
-    each(0, COMM, rim_out)
-    start(sides())
+    each(1, 2, halo_out)
+    each(0, EARLY - 1, own_out)
+    each(EARLY, COMM, rim_out)
+    start(sides_out())
     for q in range(3):
         last_table(q)
 
@@ -628,11 +628,13 @@
     ocean(0, team_drift)
     surface(state, sbuf, 0)
     row_start(1)
+    each(2, 5, halo_out)
+    each(EARLY - 1, EARLY, own_out)
+    each(5, COMM, halo_out)
     srx[b + 1] = sbuf[...]
-    each(3, COMM, halo_out)
 
     def beside(c):
-        received(halo(1, c))
+        received(halo_in(1, c))
         sides_y = []
         for sub in range(2):
             at = pl.ds(pl.multiple_of(c * size + sub * half, half), half)
@@ -655,7 +657,7 @@
 
     each(0, EARLY, beside)
     received(sides())
-    edge[1] = jnp.where(lax.rem(lane_rim, 2) == 1, exin[0], exin[1])
+    edge[1, later, :] = jnp.where(lax.rem(lane_rim[8 * EARLY :], 2) == 1, exin[0, later, :], exin[1, later, :])
     received(row_in(1))
     flow(1)
 
@@ -708,16 +710,16 @@
                 advb[at, lane_at] = value.astype(BF16)
 
     each(EARLY, COMM, give)
-    start(zonal_pair(1))
+    start(zonal_out(1))
     flow_row()
-    for part in range(KPARTS):
-        turn = advance if part < EARLY // 2 else take
-        each(2 * part, 2 * part + 2, turn)
-        multiply(part)
+    for c in range(COMM):
+        advance(c) if c < EARLY else take(c)
+        if c % 2:
+            multiply(c // 2)
     source(1, wet[...].astype(F32))
 
     stokes = dot(table[...], midb[...])
-    copies = last_pair()
+    copies = last_out()
     dbuf[0] = dot_split(stokes, otab[2, 0], otab[2, 1])
     copies[0].start()
     dbuf[1] = dot_split(stokes, otab[0, 0], otab[0, 1])
@@ -732,15 +734,16 @@
     ocean(1, last_drift)
 
     sent(beside_all())
-    sent(meta_out())
-    sent(edges_out())
+    sent(meta_in())
+    sent(edges_in())
     sent(sides())
-    sent(drift_out())
+    sent(drift_all())
     sent(last_pair())
     for step in range(STEPS):
         row_sent(step)
         sent(zonal_pair(step))
-        sent(all_out(step))
+        sent(piece_all(step))
+        sent(halo_all(step))
 
 
 def local(
@@ -804,28 +807,28 @@
         f32(2 * levels, cells),
         f32(8, points),
         f32(8, points),
-        dma((STEPS, 3)),
-        dma((STEPS, TEAM, COMM)),
-        dma((3,)),
-        dma((TEAM, EARLY)),
-        dma((STEPS, 2)),
-        dma((STEPS, 2, COMM)),
-        dma((3,)),
-        dma((TEAM,)),
+        dma((STEPS,)),
+        dma((STEPS, COMM)),
+        dma((1,)),
+        dma((EARLY,)),
+        dma((STEPS,)),
+        dma((STEPS, COMM)),
+        dma((1,)),
+        dma((1,)),
+        dma((1,)),
+        dma((1,)),
+        dma((1,)),
+        dma((1,)),
         dma((2,)),
+        dma((1,)),
         dma((2,)),
-        dma((3,)),
-        dma((TEAM,)),
-        dma((3 + TEAM,)),
-        dma((TEAM + 2,)),
-        dma((3 + TEAM,)),
-        dma((TEAM + 2,)),
-        dma((5,)),
-        dma((2 * TEAM,)),
-        dma((STEPS, 2)),
-        dma((STEPS, 2)),
+        dma((1,)),
+        dma((1,)),
         dma((2,)),
-        dma((2,)),
+        dma((STEPS,)),
+        dma((STEPS,)),
+        dma((1,)),
+        dma((1,)),
     ]
     operands = (
         spectrum,

time: 63.4 us -> 61.2 us (0.965)
  Pallas kernels: 61 us -> 58.7 us
    pallas_call x1, Pallas kernels: 61 us -> 58.7 us  [local(): pl.pallas_call(wave_kernel, out_shape=(pltpu.VMEM((comps, points), F32),...]
where the time goes in v4:
time: 61.2 us; the launch traced here: 61 us
  Pallas kernels  58.7 us (96%)
  local copies, waits for them, and re-layouts  1.6 us (3%)
  between operations  0.65 us (1%)
    pallas_call x1, Pallas kernels, local(): pl.pallas_call(wave_kernel, out_shape=(pltpu.VMEM((comps, points), F32),...  58.7 us
    unnamed x2, local copies, waits for them, and re-layouts  1.6 us

profile of v4, /device:TPU:1, one launch (start us, length us, event | category | flops | bytes accessed | tf_op | source)
XLA Modules:
  0.0 61.0 jit_solution(10547697659003323282)
XLA Ops:
  0.6 58.7 %shard_map.167 = (f32[1024,256]{1,0:T(8,128)S(1)}, f32[2,64,128]{2,1,0:T(8,128)S(1)}) custom-call(f32[1024,256]{1,0:T(8,128)} %refs_0_.1, s32[1,256]{1,0:T(1,128)} %bitcast.10, f32[2,1024]{1,0:T(2,128)} %refs_2_.1, s32[2,1024]{1,0:T(2,128)} %refs_3_.1, s32[4,2,1024]{2,1,0:T(2,128)} %bitcast.7, f32[4,2,1024]{2,1,0:T(2,128)} %bitcast.8, f32[1,1024]{1,0:T(1,128)} %bitcast.9, ...), custom_call_target="tpu_custom_call" | custom-call | tf_op jit(solution)/shard_map/pallas_call | solution.py:852
  59.4 1.0 %copy.20 = f32[1024,256]{1,0:T(8,128)} copy(f32[1024,256]{1,0:T(8,128)S(1)} %get-tuple-element.2) | data formatting | bytes 2097152
  60.3 0.6 %copy.21 = f32[2,64,128]{2,1,0:T(8,128)} copy(f32[2,64,128]{2,1,0:T(8,128)S(1)} %get-tuple-element.3) | data formatting | bytes 131072

commit v5 on v4

--- a/solution.py
+++ b/solution.py
@@ -44,7 +44,7 @@
     spec_out, cur_out,
     araw, cols, lraw, quad, pk, pk2, pkb, rx, rxb, zpk, zin, ex, exin, ce, cein, edge, adv, advb, acc, mid, midb, state,
     mbuf, meta, bmeta, osm, orx, sbuf, srx, sall, zhalo, ptab, rtab, btab, otab, dm, drx, dbuf, dhalo, dself, tan, tanr,
-    rxs, rxr, bs, br, zs, zr, es, er, fs, fr, ms, mr, os_, or_, ss, sr, ds_, dr, us, ur, hs, hr,
+    rxs, rxr, bs, br, zs, zr, es, er, fs, fr, ms, mr, os_, or_, ss, sr, ds_, dr, us, ur, hs, hr, hello,
 ):
     comps, points = spec.shape
     cells = coriolis.shape[1]
@@ -184,6 +184,9 @@
         return inner, before, after
 
     def row_start(step):
+        start(row_out(step)[0])
+
+    def row_start_outer(step):
         inner, before, after = row_out(step)
 
         @pl.when(b == 0)
@@ -193,8 +196,6 @@
         @pl.when(b == TEAM - 1)
         def _():
             start(after)
-
-        start(inner)
 
     def row_sent(step):
         src, dst, ssem, rsem = row_refs(step)
@@ -243,12 +244,15 @@
     start(loads)
     drx[TEAM : 2 * TEAM] = jnp.zeros((TEAM, levels, lanes), F32)
     barrier = pltpu.get_barrier_semaphore()
-    partners = [base + d for d in mates]
-    partners += [wrap(base - TEAM + k) for k in range(TEAM)] + [wrap(base + TEAM + k) for k in range(TEAM)]
+
+    def greet(sem, p):
+        pl.semaphore_signal(
+            sem, inc=1, device_id=(lax.div(p, dev_count), lax.rem(p, dev_count)), device_id_type=MESH
+        )
+
+    partners = [base + d for d in mates] + [ahead, behind]
     for p in partners:
-        pl.semaphore_signal(
-            barrier, inc=1, device_id=(lax.div(p, dev_count), lax.rem(p, dev_count)), device_id_type=MESH
-        )
+        greet(barrier, p)
 
     lane = lax.broadcasted_iota(jnp.int32, (half, lanes), 1)
     low = lane < width
@@ -275,6 +279,8 @@
     for load in loads:
         load.wait()
     pl.semaphore_wait(barrier, len(partners))
+    greet(hello, ahead)
+    greet(hello, behind)
 
     def pack_in(c):
         for t in range(2):
@@ -331,6 +337,8 @@
     cein[b] = ce[b]
     start(edges_out())
     each(2, COMM, pack_in)
+    pl.semaphore_wait(hello, 2)
+    row_start_outer(0)
     start(zonal_out(0))
     araw[...] = jnp.zeros_like(araw)
     araw[0:2, :] = courant[...]
@@ -601,7 +609,7 @@
         start(piece_out(1, c))
         rx[1, b, halves(c), :] = pk2[b, halves(c), :]
 
-    each(1, 2, halo_out)
+    each(1, 3, halo_out)
     each(0, EARLY - 1, own_out)
     each(EARLY, COMM, rim_out)
     start(sides_out())
@@ -627,8 +635,9 @@
 
     ocean(0, team_drift)
     surface(state, sbuf, 0)
+    row_start_outer(1)
     row_start(1)
-    each(2, 5, halo_out)
+    each(3, 5, halo_out)
     each(EARLY - 1, EARLY, own_out)
     each(5, COMM, halo_out)
     srx[b + 1] = sbuf[...]
@@ -829,6 +838,7 @@
         dma((STEPS,)),
         dma((1,)),
         dma((1,)),
+        pltpu.SemaphoreType.REGULAR,
     ]
     operands = (
         spectrum,

time: 61.2 us -> 59.8 us (0.977)
  Pallas kernels: 58.7 us -> 57.4 us
    pallas_call x1, Pallas kernels: 58.7 us -> 57.4 us  [local(): pl.pallas_call(wave_kernel, out_shape=(pltpu.VMEM((comps, points), F32),...]
where the time goes in v5:
time: 59.8 us; the launch traced here: 59.6 us
  Pallas kernels  57.4 us (96%)
  local copies, waits for them, and re-layouts  1.6 us (3%)
  between operations  0.65 us (1%)
    pallas_call x1, Pallas kernels, local(): pl.pallas_call(wave_kernel, out_shape=(pltpu.VMEM((comps, points), F32),...  57.4 us
    unnamed x2, local copies, waits for them, and re-layouts  1.6 us

profile of v5, /device:TPU:1, one launch (start us, length us, event | category | flops | bytes accessed | tf_op | source)
XLA Modules:
  0.0 59.6 jit_solution(2044073941848498706)
XLA Ops:
  0.6 57.4 %shard_map.167 = (f32[1024,256]{1,0:T(8,128)S(1)}, f32[2,64,128]{2,1,0:T(8,128)S(1)}) custom-call(f32[1024,256]{1,0:T(8,128)} %refs_0_.1, s32[1,256]{1,0:T(1,128)} %bitcast.10, f32[2,1024]{1,0:T(2,128)} %refs_2_.1, s32[2,1024]{1,0:T(2,128)} %refs_3_.1, s32[4,2,1024]{2,1,0:T(2,128)} %bitcast.7, f32[4,2,1024]{2,1,0:T(2,128)} %bitcast.8, f32[1,1024]{1,0:T(1,128)} %bitcast.9, ...), custom_call_target="tpu_custom_call" | custom-call | tf_op jit(solution)/shard_map/pallas_call | solution.py:862
  58.0 1.0 %copy.20 = f32[1024,256]{1,0:T(8,128)} copy(f32[1024,256]{1,0:T(8,128)S(1)} %get-tuple-element.2) | data formatting | bytes 2097152
  59.0 0.6 %copy.21 = f32[2,64,128]{2,1,0:T(8,128)} copy(f32[2,64,128]{2,1,0:T(8,128)S(1)} %get-tuple-element.3) | data formatting | bytes 131072

commit v6 on v5

--- a/solution.py
+++ b/solution.py
@@ -9,7 +9,7 @@
 OCEAN_STEP = 0.5
 TEAM = 4
 COMM = 8
-EARLY = 3
+EARLY = 2
 INPUTS = 16
 KPARTS = 4
 MESH = pl.DeviceIdType.MESH
@@ -26,14 +26,19 @@
 
 
 def dot_split(x, table_high, table_low):
+    rows = x.shape[0]
     high, low = split(x)
-    return dot(high, table_high) + (dot(low, table_high) + dot(high, table_low))
+    main = dot(jnp.concatenate([high, low], axis=0), table_high)
+    return main[0:rows] + (main[rows:] + dot(high, table_low))
 
 
 def wave_kernel(*refs):
     given, (spec_out, cur_out), scratch = refs[:INPUTS], refs[INPUTS : INPUTS + 2], refs[INPUTS + 2 :]
     copied, load_sems, rest = scratch[:INPUTS], scratch[INPUTS], scratch[INPUTS + 1 :]
-    loads = [pltpu.make_async_copy(a, c, load_sems.at[i]) for i, (a, c) in enumerate(zip(given, copied))]
+    head = given[0].shape[0] // COMM
+    pairs = [(given[0].at[0:head], copied[0].at[0:head])] + list(zip(given[1:], copied[1:]))
+    pairs.append((given[0].at[head:], copied[0].at[head:]))
+    loads = [pltpu.make_async_copy(a, c, load_sems.at[i]) for i, (a, c) in enumerate(pairs)]
     wave_body(loads, *copied, spec_out, cur_out, *rest)
 
 
@@ -276,8 +281,7 @@
             out = jnp.where(here, pltpu.roll(part, 4 * g, 1) if g else part, out)
         return out
 
-    for load in loads:
-        load.wait()
+    loads[0].wait()
     pl.semaphore_wait(barrier, len(partners))
     greet(hello, ahead)
     greet(hello, behind)
@@ -292,6 +296,8 @@
         start(piece_out(0, c))
 
     each(0, 1, pack_in)
+    for load in loads[1:]:
+        load.wait()
     lraw[...] = jnp.zeros_like(lraw)
     lraw[0:1, 0:levels] = mixing[...]
     lraw[1:2, 0:levels] = sweight[...]
@@ -610,7 +616,7 @@
         rx[1, b, halves(c), :] = pk2[b, halves(c), :]
 
     each(1, 3, halo_out)
-    each(0, EARLY - 1, own_out)
+    each(0, EARLY, own_out)
     each(EARLY, COMM, rim_out)
     start(sides_out())
     for q in range(3):
@@ -638,7 +644,6 @@
     row_start_outer(1)
     row_start(1)
     each(3, 5, halo_out)
-    each(EARLY - 1, EARLY, own_out)
     each(5, COMM, halo_out)
     srx[b + 1] = sbuf[...]
 
@@ -719,9 +724,10 @@
                 advb[at, lane_at] = value.astype(BF16)
 
     each(EARLY, COMM, give)
-    start(zonal_out(1))
     flow_row()
     for c in range(COMM):
+        if c == COMM - 2:
+            start(zonal_out(1))
         advance(c) if c < EARLY else take(c)
         if c % 2:
             multiply(c // 2)
@@ -858,7 +864,7 @@
         mixing.reshape(1, levels),
         surface_weights.reshape(1, levels),
     )
-    scratch = [pltpu.VMEM(x.shape, x.dtype) for x in operands] + [dma((INPUTS,))] + scratch
+    scratch = [pltpu.VMEM(x.shape, x.dtype) for x in operands] + [dma((INPUTS + 1,))] + scratch
     return pl.pallas_call(
         wave_kernel,
         out_shape=(

time: 59.8 us -> 58.1 us (0.972)
  Pallas kernels: 57.4 us -> 55.7 us
    pallas_call x1, Pallas kernels: 57.4 us -> 55.7 us  [local(): pl.pallas_call(wave_kernel, out_shape=(pltpu.VMEM((comps, points), F32),...]
where the time goes in v6:
time: 58.1 us; the launch traced here: 58 us
  Pallas kernels  55.7 us (96%)
  local copies, waits for them, and re-layouts  1.6 us (3%)
  between operations  0.65 us (1%)
    pallas_call x1, Pallas kernels, local(): pl.pallas_call(wave_kernel, out_shape=(pltpu.VMEM((comps, points), F32),...  55.7 us
    unnamed x2, local copies, waits for them, and re-layouts  1.6 us

profile of v6, /device:TPU:1, one launch (start us, length us, event | category | flops | bytes accessed | tf_op | source)
XLA Modules:
  0.0 58.0 jit_solution(4826583081391457766)
XLA Ops:
  0.6 55.7 %shard_map.167 = (f32[1024,256]{1,0:T(8,128)S(1)}, f32[2,64,128]{2,1,0:T(8,128)S(1)}) custom-call(f32[1024,256]{1,0:T(8,128)} %refs_0_.1, s32[1,256]{1,0:T(1,128)} %bitcast.10, f32[2,1024]{1,0:T(2,128)} %refs_2_.1, s32[2,1024]{1,0:T(2,128)} %refs_3_.1, s32[4,2,1024]{2,1,0:T(2,128)} %bitcast.7, f32[4,2,1024]{2,1,0:T(2,128)} %bitcast.8, f32[1,1024]{1,0:T(1,128)} %bitcast.9, ...), custom_call_target="tpu_custom_call" | custom-call | tf_op jit(solution)/shard_map/pallas_call | solution.py:868
  56.4 1.0 %copy.20 = f32[1024,256]{1,0:T(8,128)} copy(f32[1024,256]{1,0:T(8,128)S(1)} %get-tuple-element.2) | data formatting | bytes 2097152
  57.3 0.6 %copy.21 = f32[2,64,128]{2,1,0:T(8,128)} copy(f32[2,64,128]{2,1,0:T(8,128)S(1)} %get-tuple-element.3) | data formatting | bytes 131072

commit v7 on v6

--- a/solution.py
+++ b/solution.py
@@ -219,7 +219,7 @@
             remote(dm.at[0], drx.at[TEAM + b], ds_.at[0], dr.at[1], wrap(base - 1)),
             remote(dm.at[TEAM + 1], drx.at[TEAM + b], ds_.at[0], dr.at[1], wrap(base + TEAM)),
         ]
-        return copies + [remote(dm.at[d + 1], drx.at[b], ds_.at[0], dr.at[0], base + d) for d in mates]
+        return [remote(dm.at[d + 1], drx.at[b], ds_.at[0], dr.at[0], base + d) for d in mates] + copies
 
     def drift_all():
         return gather(dm, drx, ds_.at[0], dr.at[0], TEAM + 1)
@@ -247,7 +247,7 @@
         return [remote(dbuf, dhalo, hs.at[0], hr.at[0], up)]
 
     start(loads)
-    drx[TEAM : 2 * TEAM] = jnp.zeros((TEAM, levels, lanes), F32)
+    drx[TEAM : 2 * TEAM] = jnp.zeros((TEAM,) + drx.shape[1:], F32)
     barrier = pltpu.get_barrier_semaphore()
 
     def greet(sem, p):
@@ -269,6 +269,11 @@
         return jnp.where(low, pltpu.roll(a, width, 1), c)
 
     lane_row = lax.broadcasted_iota(jnp.int32, (8, lanes), 1)
+    fold = drx.shape[1]
+    third = lanes // 3
+    margin = (third - window - 2) // 2
+    lane_fold = lane[0:fold]
+    in_first, in_second, in_third = lane_fold < third, lane_fold < 2 * third, lane_fold < 3 * third
     wide_lane = lax.broadcasted_iota(jnp.int32, (size, lanes), 1)
     rim = lax.rem(wide_lane + 1, width) < 2
 
@@ -399,7 +404,7 @@
             value = value + jnp.where(bmeta[j : j + 1, :] - owner == slots, bmeta[4 + j : 5 + j, :], 0.0)
         ptab[0, q * cells : (q + 1) * cells, :], ptab[1, q * cells : (q + 1) * cells, :] = split(value)
 
-    shift = lax.rem(cells + window // 2 - window * b, cells)
+    shift = lax.rem(cells + margin - window * b, cells)
     pointer = lax.broadcasted_iota(jnp.int32, (width, cells), 0).astype(F32)
     for t in range((TEAM + 2) // 2):
         near = pltpu.roll(orx[2 * t, 0:8], shift, 1)
@@ -601,9 +606,14 @@
     stokes = dot(table[...], midb[...])
     parts = dot_split(stokes, btab[0], btab[1])
     for t in range((TEAM + 2) // 2):
-        zonal = parts[0:levels, t * lanes : (t + 1) * lanes]
-        merid = parts[levels : 2 * levels, t * lanes : (t + 1) * lanes]
-        dm[2 * t], dm[2 * t + 1] = even(zonal, merid), odd(zonal, merid)
+        tile = parts[:, t * lanes : (t + 1) * lanes]
+        rest = jnp.concatenate([tile[2 * fold :], jnp.zeros((3 * fold - 2 * levels, lanes), F32)], axis=0)
+        for k in range(2):
+            first, second, last_rows = (
+                pltpu.roll(x, (i * third - k * width) % lanes, 1) if i or k else x
+                for i, x in enumerate((tile[0:fold], tile[fold : 2 * fold], rest))
+            )
+            dm[2 * t + k] = jnp.where(in_first, first, jnp.where(in_second, second, last_rows))
     start(drift_out())
     drx[b] = dm[b + 1]
     def own_out(c):
@@ -630,14 +640,20 @@
         def _():
             received(outer)
 
-        drift_x = jnp.zeros((levels, cells), F32)
-        drift_y = jnp.zeros((levels, cells), F32)
+        sums = [jnp.zeros((fold, cells), F32)] * 3
         for s in range(TEAM):
             part = drx[s] + drx[TEAM + s]
-            to = (window * s - window // 2) % cells
-            drift_x += pltpu.roll(jnp.where(low, part, 0.0), to, 1)
-            drift_y += pltpu.roll(jnp.where(low, pltpu.roll(part, width, 1), 0.0), to, 1)
-        return drift_x, drift_y
+            picks = (
+                jnp.where(in_first, part, 0.0),
+                jnp.where(in_second & ~in_first, part, 0.0),
+                jnp.where(in_third & ~in_second, part, 0.0),
+            )
+            sums = [
+                total_part + pltpu.roll(x, (window * s - margin - i * third) % cells, 1)
+                for i, (total_part, x) in enumerate(zip(sums, picks))
+            ]
+        drift = jnp.concatenate([sums[0], sums[1], sums[2][0 : 2 * levels - 2 * fold]], axis=0)
+        return drift[0:levels], drift[levels : 2 * levels]
 
     ocean(0, team_drift)
     surface(state, sbuf, 0)
@@ -770,6 +786,7 @@
     lanes = points // 2
     packed = comps // 2
     rim = comps // 16
+    fold = -(-2 * levels // 24) * 8
     vm = pl.BlockSpec(memory_space=pltpu.VMEM)
     dma = pltpu.SemaphoreType.DMA
 
@@ -815,8 +832,8 @@
         bf16(2, 3 * cells, points),
         bf16(2, points, (TEAM + 2) // 2 * lanes),
         bf16(3, 2, points, cells),
-        f32(TEAM + 2, levels, lanes),
-        f32(2 * TEAM, levels, lanes),
+        f32(TEAM + 2, fold, lanes),
+        f32(2 * TEAM, fold, lanes),
         f32(2, 2 * levels, cells),
         f32(2, 2 * levels, cells),
         f32(2 * levels, cells),

time: 58.1 us -> 57.8 us (level)
  no operation moved by 1% of the time
where the time goes in v7:
time: 57.8 us; the launch traced here: 57.7 us
  Pallas kernels  55.4 us (96%)
  local copies, waits for them, and re-layouts  1.6 us (3%)
  between operations  0.65 us (1%)
    pallas_call x1, Pallas kernels, local(): pl.pallas_call(wave_kernel, out_shape=(pltpu.VMEM((comps, points), F32),...  55.4 us
    unnamed x2, local copies, waits for them, and re-layouts  1.6 us

profile of v7, /device:TPU:1, one launch (start us, length us, event | category | flops | bytes accessed | tf_op | source)
XLA Modules:
  0.0 57.7 jit_solution(9747340810859245053)
XLA Ops:
  0.6 55.4 %shard_map.167 = (f32[1024,256]{1,0:T(8,128)S(1)}, f32[2,64,128]{2,1,0:T(8,128)S(1)}) custom-call(f32[1024,256]{1,0:T(8,128)} %refs_0_.1, s32[1,256]{1,0:T(1,128)} %bitcast.10, f32[2,1024]{1,0:T(2,128)} %refs_2_.1, s32[2,1024]{1,0:T(2,128)} %refs_3_.1, s32[4,2,1024]{2,1,0:T(2,128)} %bitcast.7, f32[4,2,1024]{2,1,0:T(2,128)} %bitcast.8, f32[1,1024]{1,0:T(1,128)} %bitcast.9, ...), custom_call_target="tpu_custom_call" | custom-call | tf_op jit(solution)/shard_map/pallas_call | solution.py:885
  56.1 1.0 %copy.20 = f32[1024,256]{1,0:T(8,128)} copy(f32[1024,256]{1,0:T(8,128)S(1)} %get-tuple-element.2) | data formatting | bytes 2097152
  57.0 0.6 %copy.21 = f32[2,64,128]{2,1,0:T(8,128)} copy(f32[2,64,128]{2,1,0:T(8,128)S(1)} %get-tuple-element.3) | data formatting | bytes 131072
